TPU v7x, 32 devices: a whole 2x2x4 slice. The times are simulated.
32 devices in a mesh: fsdp: 32 (over z, y, x, core).
Axes of the slice: x: 2, y: 2, z: 4, core: 2. Of those that a mesh axis runs over, the one named last changes fastest.
Arguments:
- w_query: float32 [2, 960, 960], P(None, 'fsdp')
- w_key: float32 [2, 960, 320], P(None, 'fsdp')
- w_value: float32 [2, 960, 320], P(None, 'fsdp')
- w_out: float32 [2, 960, 960], P(None, 'fsdp')
- w_gate: float32 [2, 960, 2560], P(None, 'fsdp')
- w_up: float32 [2, 960, 2560], P(None, 'fsdp')
- w_down: float32 [2, 2560, 960], P(None, 'fsdp')
- gain_attn: float32 [2, 960], P(None, 'fsdp')
- gain_mlp: float32 [2, 960], P(None, 'fsdp')
- rope_cos: float32 [128, 32], replicated
- rope_sin: float32 [128, 32], replicated
- x_in: bfloat16 [256, 128, 960], P('fsdp')
- y_cot: bfloat16 [256, 128, 960], P('fsdp')
Outputs:
- output 1: bfloat16 [256, 128, 960], P('fsdp')
- output 2: bfloat16 [256, 128, 960], P('fsdp')
- output 3: float32 [2, 960, 960], P(None, 'fsdp')
- output 4: float32 [2, 960, 320], P(None, 'fsdp')
- output 5: float32 [2, 960, 320], P(None, 'fsdp')
- output 6: float32 [2, 960, 960], P(None, 'fsdp')
- output 7: float32 [2, 960, 2560], P(None, 'fsdp')
- output 8: float32 [2, 960, 2560], P(None, 'fsdp')
- output 9: float32 [2, 2560, 960], P(None, 'fsdp')
- output 10: float32 [2, 960], P(None, 'fsdp')
- output 11: float32 [2, 960], P(None, 'fsdp')
All inputs are finite; a program needn't handle non-finite values.
Results may differ from a plain program's by a relative error of at most 0.02.
Values are sent between devices in bfloat16 or wider.
A program may use at most 1 GiB of HBM per device.

v0:
```python
import jax
import jax.numpy as jnp
from jax import lax
from jax.sharding import PartitionSpec as P

NORM_EPS = 1e-5
MASK_VALUE = -1e30


def rms_forward(values, gain):
    vals32 = values.astype(jnp.float32)
    inv_rms = lax.rsqrt(jnp.mean(vals32 * vals32, axis=-1, keepdims=True) + NORM_EPS)
    normed = (vals32 * inv_rms * gain.astype(jnp.float32)).astype(jnp.bfloat16)
    return normed, inv_rms


def rms_backward(values, inv_rms, gain, grad_normed):
    scaled = values.astype(jnp.float32) * inv_rms
    grad_scaled = grad_normed * gain.astype(jnp.float32)
    grad_gain = jnp.sum(grad_normed * scaled, axis=(0, 1))
    grad_values = inv_rms * (grad_scaled - scaled * jnp.mean(grad_scaled * scaled, axis=-1, keepdims=True))
    return grad_values, grad_gain


def rotary(heads32, rope_cos, rope_sin, sin_sign):
    half_dim = rope_cos.shape[-1]
    first_half = heads32[..., :half_dim]
    second_half = heads32[..., half_dim:]
    cos_b = rope_cos[None, :, None, :]
    sin_b = sin_sign * rope_sin[None, :, None, :]
    return jnp.concatenate([first_half * cos_b - second_half * sin_b, second_half * cos_b + first_half * sin_b], axis=-1)


def layer_forward(weights, rope_cos, rope_sin, hidden):
    w_query, w_key, w_value, w_out, w_gate, w_up, w_down, gain_attn, gain_mlp = weights
    batch_size = hidden.shape[0]
    seq_len = hidden.shape[1]
    head_dim = 2 * rope_cos.shape[-1]
    kv_heads = w_key.shape[1] // head_dim
    num_heads = w_query.shape[1] // head_dim
    group_size = num_heads // kv_heads
    normed, inv_rms_attn = rms_forward(hidden, gain_attn)
    q_proj = jnp.einsum("bsd,df->bsf", normed, w_query, preferred_element_type=jnp.float32)
    q_heads = rotary(q_proj.reshape(batch_size, seq_len, num_heads, head_dim), rope_cos, rope_sin, 1.0)
    q_heads = q_heads.astype(jnp.bfloat16).reshape(batch_size, seq_len, kv_heads, group_size, head_dim)
    k_proj = jnp.einsum("bsd,df->bsf", normed, w_key, preferred_element_type=jnp.float32)
    k_heads = rotary(k_proj.reshape(batch_size, seq_len, kv_heads, head_dim), rope_cos, rope_sin, 1.0).astype(jnp.bfloat16)
    v_heads = jnp.einsum("bsd,df->bsf", normed, w_value, preferred_element_type=jnp.float32)
    v_heads = v_heads.astype(jnp.bfloat16).reshape(batch_size, seq_len, kv_heads, head_dim)
    scores = jnp.einsum("bqkgd,bskd->bkgqs", q_heads, k_heads, preferred_element_type=jnp.float32) * head_dim ** -0.5
    positions = jnp.arange(seq_len)
    scores = jnp.where(positions[:, None] >= positions[None, :], scores, MASK_VALUE)
    attn_probs = jax.nn.softmax(scores, axis=-1).astype(jnp.bfloat16)
    attn_heads = jnp.einsum("bkgqs,bskd->bqkgd", attn_probs, v_heads, preferred_element_type=jnp.float32)
    attn_heads = attn_heads.astype(jnp.bfloat16).reshape(batch_size, seq_len, num_heads * head_dim)
    attn_proj = jnp.einsum("bsf,fd->bsd", attn_heads, w_out, preferred_element_type=jnp.float32)
    mid_hidden = (hidden.astype(jnp.float32) + attn_proj).astype(jnp.bfloat16)
    normed_mlp, inv_rms_mlp = rms_forward(mid_hidden, gain_mlp)
    gate_pre = jnp.einsum("bsd,df->bsf", normed_mlp, w_gate, preferred_element_type=jnp.float32)
    up_proj = jnp.einsum("bsd,df->bsf", normed_mlp, w_up, preferred_element_type=jnp.float32)
    mlp_act = (jax.nn.silu(gate_pre) * up_proj).astype(jnp.bfloat16)
    down_proj = jnp.einsum("bsf,fd->bsd", mlp_act, w_down, preferred_element_type=jnp.float32)
    out_hidden = (mid_hidden.astype(jnp.float32) + down_proj).astype(jnp.bfloat16)
    saved_acts = (hidden, inv_rms_attn, normed, q_heads, k_heads, v_heads, attn_probs, attn_heads, mid_hidden, inv_rms_mlp, normed_mlp, gate_pre, up_proj, mlp_act)
    return out_hidden, saved_acts


def layer_backward(weights, rope_cos, rope_sin, saved_acts, grad_out):
    w_query, w_key, w_value, w_out, w_gate, w_up, w_down, gain_attn, gain_mlp = weights
    (hidden, inv_rms_attn, normed, q_heads, k_heads, v_heads, attn_probs, attn_heads, mid_hidden, inv_rms_mlp, normed_mlp, gate_pre, up_proj, mlp_act) = saved_acts
    batch_size = hidden.shape[0]
    seq_len = hidden.shape[1]
    head_dim = 2 * rope_cos.shape[-1]
    kv_heads = k_heads.shape[2]
    num_heads = kv_heads * q_heads.shape[3]
    grad_w_down = jnp.einsum("bsf,bsd->fd", mlp_act, grad_out, preferred_element_type=jnp.float32)
    grad_act = jnp.einsum("bsd,fd->bsf", grad_out, w_down, preferred_element_type=jnp.float32)
    gate_sig = jax.nn.sigmoid(gate_pre)
    grad_up = (grad_act * gate_pre * gate_sig).astype(jnp.bfloat16)
    grad_gate = (grad_act * up_proj * gate_sig * (1.0 + gate_pre * (1.0 - gate_sig))).astype(jnp.bfloat16)
    grad_w_gate = jnp.einsum("bsd,bsf->df", normed_mlp, grad_gate, preferred_element_type=jnp.float32)
    grad_w_up = jnp.einsum("bsd,bsf->df", normed_mlp, grad_up, preferred_element_type=jnp.float32)
    grad_normed_mlp = (jnp.einsum("bsf,df->bsd", grad_gate, w_gate, preferred_element_type=jnp.float32)
                       + jnp.einsum("bsf,df->bsd", grad_up, w_up, preferred_element_type=jnp.float32))
    grad_mid_norm, grad_gain_mlp = rms_backward(mid_hidden, inv_rms_mlp, gain_mlp, grad_normed_mlp)
    grad_mid = grad_out.astype(jnp.float32) + grad_mid_norm
    grad_mid_bf = grad_mid.astype(jnp.bfloat16)
    grad_w_out = jnp.einsum("bsf,bsd->fd", attn_heads, grad_mid_bf, preferred_element_type=jnp.float32)
    grad_attn = jnp.einsum("bsd,fd->bsf", grad_mid_bf, w_out, preferred_element_type=jnp.float32)
    grad_attn = grad_attn.astype(jnp.bfloat16).reshape(batch_size, seq_len, kv_heads, -1, head_dim)
    grad_v = jnp.einsum("bkgqs,bqkgd->bskd", attn_probs, grad_attn, preferred_element_type=jnp.float32)
    grad_v = grad_v.astype(jnp.bfloat16).reshape(batch_size, seq_len, -1)
    grad_probs = jnp.einsum("bqkgd,bskd->bkgqs", grad_attn, v_heads, preferred_element_type=jnp.float32)
    probs32 = attn_probs.astype(jnp.float32)
    grad_scores = probs32 * (grad_probs - jnp.sum(probs32 * grad_probs, axis=-1, keepdims=True)) * head_dim ** -0.5
    grad_scores = grad_scores.astype(jnp.bfloat16)
    grad_q = jnp.einsum("bkgqs,bskd->bqkgd", grad_scores, k_heads, preferred_element_type=jnp.float32)
    grad_q = rotary(grad_q.reshape(batch_size, seq_len, num_heads, head_dim), rope_cos, rope_sin, -1.0)
    grad_q = grad_q.astype(jnp.bfloat16).reshape(batch_size, seq_len, -1)
    grad_k = jnp.einsum("bkgqs,bqkgd->bskd", grad_scores, q_heads, preferred_element_type=jnp.float32)
    grad_k = rotary(grad_k, rope_cos, rope_sin, -1.0).astype(jnp.bfloat16).reshape(batch_size, seq_len, -1)
    grad_w_query = jnp.einsum("bsd,bsf->df", normed, grad_q, preferred_element_type=jnp.float32)
    grad_w_key = jnp.einsum("bsd,bsf->df", normed, grad_k, preferred_element_type=jnp.float32)
    grad_w_value = jnp.einsum("bsd,bsf->df", normed, grad_v, preferred_element_type=jnp.float32)
    grad_normed = (jnp.einsum("bsf,df->bsd", grad_q, w_query, preferred_element_type=jnp.float32)
                   + jnp.einsum("bsf,df->bsd", grad_k, w_key, preferred_element_type=jnp.float32)
                   + jnp.einsum("bsf,df->bsd", grad_v, w_value, preferred_element_type=jnp.float32))
    grad_hidden_norm, grad_gain_attn = rms_backward(hidden, inv_rms_attn, gain_attn, grad_normed)
    grad_hidden = (grad_mid + grad_hidden_norm).astype(jnp.bfloat16)
    layer_grads = (grad_w_query, grad_w_key, grad_w_value, grad_w_out, grad_w_gate, grad_w_up, grad_w_down, grad_gain_attn, grad_gain_mlp)
    return grad_hidden, layer_grads


def solution(mesh):
    shard_spec = P(None, "fsdp")
    batch_spec = P("fsdp")

    def gather_layer(masters, layer_idx):
        return tuple(lax.all_gather(master[layer_idx].astype(jnp.bfloat16), "fsdp", axis=0, tiled=True) for master in masters)

    def local_step(w_query, w_key, w_value, w_out, w_gate, w_up, w_down, gain_attn, gain_mlp, rope_cos, rope_sin, x_in, y_cot):
        masters = (w_query, w_key, w_value, w_out, w_gate, w_up, w_down, gain_attn, gain_mlp)
        num_layers = w_query.shape[0]
        hidden = x_in
        saved_layers = []
        for layer_idx in range(num_layers):
            weights = gather_layer(masters, layer_idx)
            hidden, saved_acts = layer_forward(weights, rope_cos, rope_sin, hidden)
            saved_layers.append(saved_acts)
        masters, saved_layers, hidden = lax.optimization_barrier((masters, saved_layers, hidden))
        grad_hidden = y_cot
        grad_layers = []
        for layer_idx in reversed(range(num_layers)):
            weights = gather_layer(masters, layer_idx)
            grad_hidden, layer_grads = layer_backward(weights, rope_cos, rope_sin, saved_layers[layer_idx], grad_hidden)
            grad_layers.insert(0, tuple(lax.psum_scatter(grad_full, "fsdp", scatter_dimension=0, tiled=True) for grad_full in layer_grads))
        grad_stacked = tuple(jnp.stack([layer_part[tensor_idx] for layer_part in grad_layers]) for tensor_idx in range(len(masters)))
        return (hidden, grad_hidden) + grad_stacked

    in_specs = (shard_spec,) * 9 + (P(), P(), batch_spec, batch_spec)
    out_specs = (batch_spec, batch_spec) + (shard_spec,) * 9
    return jax.shard_map(local_step, mesh=mesh, in_specs=in_specs, out_specs=out_specs, check_vma=False)
```

profile of v0, /device:TPU:1, one launch (start us, length us, event | category | flops | bytes accessed | tf_op | source)
XLA Modules:
  0.0 2639.0 jit_solution(6471453145971075970)
XLA Ops:
  20.8 42.8 %all-reduce.38 = (bf16[960]{0:T(1024)(128)(2,1)S(1)}, bf16[960]{0:T(1024)(128)(2,1)}, bf16[960]{0:T(1024)(128)(2,1)}, bf16[960]{0:T(1024)(128)(2,1)}) all-reduce(bf16[960]{0:T(1024)(128)(2,1)S(1)} %dynamic-update-slice, bf16[960]{0:T(1024)(128)(2,1)S(1)} %dynamic-update-slice.1, ...), channel_id=2, replica_groups=mesh['fsdp'=32] {'fsdp'}, use_global_device_ids=true, to_apply=%add | all-reduce | flops 3840 | bytes 15360
  65.9 45.2 %all-gather.2 = bf16[1,960,320]{2,0,1:T(2,128)(2,1)S(1)} all-gather(bf16[1,30,320]{2,0,1:T(2,128)(2,1)S(1)} %get-tuple-element.211), channel_id=4, replica_groups=mesh['fsdp'=32] {'fsdp'}, dimensions={1}, use_global_device_ids=true | all-gather | bytes 633600 | tf_op jit(solution)/shard_map/all_gather | solution.py:119
  114.6 41.8 %all-gather.3 = bf16[1,960,320]{2,0,1:T(2,128)(2,1)S(1)} all-gather(bf16[1,30,320]{2,0,1:T(2,128)(2,1)S(1)} %get-tuple-element.209), channel_id=5, replica_groups=mesh['fsdp'=32] {'fsdp'}, dimensions={1}, use_global_device_ids=true | all-gather | bytes 633600 | tf_op jit(solution)/shard_map/all_gather | solution.py:119
  164.8 46.7 %all-gather.11 = bf16[1,960,320]{2,0,1:T(2,128)(2,1)S(1)} all-gather(bf16[1,30,320]{2,0,1:T(2,128)(2,1)S(1)} %copy-done.73), channel_id=13, replica_groups=mesh['fsdp'=32] {'fsdp'}, dimensions={1}, use_global_device_ids=true | all-gather | bytes 633600 | tf_op jit(solution)/shard_map/all_gather | solution.py:119
  214.9 43.2 %all-gather.12 = bf16[1,960,320]{2,0,1:T(2,128)(2,1)S(1)} all-gather(bf16[1,30,320]{2,0,1:T(2,128)(2,1)S(1)} %get-tuple-element.208), channel_id=14, replica_groups=mesh['fsdp'=32] {'fsdp'}, dimensions={1}, use_global_device_ids=true | all-gather | bytes 633600 | tf_op jit(solution)/shard_map/all_gather | solution.py:119
  264.0 10.5 copy.88
  289.6 10.5 copy.92
  306.5 10.7 copy.94
  317.2 10.5 copy.98
  327.7 32.2 %all-gather.61.cloned.1.call-done = bf16[1,960,2560]{2,0,1:T(2,128)(2,1)} async-done(((bf16[1,30,2560]{2,0,1:T(2,128)(2,1)}), bf16[1,960,2560]{2,0,1:T(2,128)(2,1)}) %all-gather.61.cloned.1.call-update) | async-done | bytes 4915216 | tf_op jit(solution)/shard_map/all_gather | solution.py:119
  359.9 12.2 fusion.58
  372.1 73.0 %all-gather.63.cloned.1.call-done = bf16[1,960,2560]{2,0,1:T(2,128)(2,1)} async-done(((bf16[1,30,2560]{2,0,1:T(2,128)(2,1)}), bf16[1,960,2560]{2,0,1:T(2,128)(2,1)}) %all-gather.63.cloned.1.call-update) | async-done | bytes 4915216 | tf_op jit(solution)/shard_map/all_gather | solution.py:119
  445.1 16.0 multiply_convert_fusion.3
  461.1 52.2 %all-gather.65.cloned.1.call-done = bf16[1,2560,960]{2,1,0:T(8,128)(2,1)} async-done(((bf16[1,80,960]{2,1,0:T(8,128)(2,1)}), bf16[1,2560,960]{2,1,0:T(8,128)(2,1)}) %all-gather.65.cloned.1.call-update) | async-done | bytes 4915216 | tf_op jit(solution)/shard_map/all_gather | solution.py:119
  513.2 9.6 fusion.69
  545.4 53.2 %all-gather.71.cloned.1.call-done = bf16[1,960,2560]{2,0,1:T(2,128)(2,1)} async-done(((bf16[1,30,2560]{2,0,1:T(2,128)(2,1)}), bf16[1,960,2560]{2,0,1:T(2,128)(2,1)}) %all-gather.71.cloned.1.call-update) | async-done | bytes 4915216 | tf_op jit(solution)/shard_map/all_gather | solution.py:119
  598.6 11.5 fusion.52
  610.1 73.8 %all-gather.73.cloned.1.call-done = bf16[1,960,2560]{2,0,1:T(2,128)(2,1)} async-done(((bf16[1,30,2560]{2,0,1:T(2,128)(2,1)}), bf16[1,960,2560]{2,0,1:T(2,128)(2,1)}) %all-gather.73.cloned.1.call-update) | async-done | bytes 4915216 | tf_op jit(solution)/shard_map/all_gather | solution.py:119
  683.9 15.1 multiply_convert_fusion.2
  699.0 52.9 %all-gather.75.cloned.1.call-done = bf16[1,2560,960]{2,1,0:T(8,128)(2,1)} async-done(((bf16[1,80,960]{2,1,0:T(8,128)(2,1)}), bf16[1,2560,960]{2,1,0:T(8,128)(2,1)}) %all-gather.75.cloned.1.call-update) | async-done | bytes 4915216 | tf_op jit(solution)/shard_map/all_gather | solution.py:119
  751.9 10.1 fusion.76
  771.6 39.6 %all-reduce.37 = (bf16[960]{0:T(1024)(128)(2,1)S(1)}, bf16[960]{0:T(1024)(128)(2,1)S(1)}, bf16[960]{0:T(1024)(128)(2,1)S(1)}, bf16[960]{0:T(1024)(128)(2,1)S(1)}) all-reduce(bf16[960]{0:T(1024)(128)(2,1)S(1)} %dynamic-update-slice.4, bf16[960]{0:T(1024)(128)(2,1)S(1)} %dynamic-update-slice.5, ...), channel_id=23, replica_groups=mesh['fsdp'=32] {'fsdp'}, use_global_device_ids=true, to_apply=%add.4 | all-reduce | flops 3840 | bytes 15360
  811.4 47.3 %all-gather.24 = bf16[1,960,320]{2,0,1:T(2,128)(2,1)S(1)} all-gather(bf16[1,30,320]{2,0,1:T(2,128)(2,1)S(1)} %get-tuple-element.207), channel_id=26, replica_groups=mesh['fsdp'=32] {'fsdp'}, dimensions={1}, use_global_device_ids=true | all-gather | bytes 633600 | tf_op jit(solution)/shard_map/all_gather | solution.py:119
  863.7 46.7 %all-gather.25 = bf16[1,960,320]{2,0,1:T(2,128)(2,1)S(1)} all-gather(bf16[1,30,320]{2,0,1:T(2,128)(2,1)S(1)} %get-tuple-element.205), channel_id=27, replica_groups=mesh['fsdp'=32] {'fsdp'}, dimensions={1}, use_global_device_ids=true | all-gather | bytes 633600 | tf_op jit(solution)/shard_map/all_gather | solution.py:119
  913.8 45.6 %all-gather.33 = bf16[1,960,320]{2,0,1:T(2,128)(2,1)S(1)} all-gather(bf16[1,30,320]{2,0,1:T(2,128)(2,1)S(1)} %get-tuple-element.206), channel_id=35, replica_groups=mesh['fsdp'=32] {'fsdp'}, dimensions={1}, use_global_device_ids=true | all-gather | bytes 633600 | tf_op jit(solution)/shard_map/all_gather | solution.py:119
  962.9 47.0 %all-gather.34 = bf16[1,960,320]{2,0,1:T(2,128)(2,1)S(1)} all-gather(bf16[1,30,320]{2,0,1:T(2,128)(2,1)} %get-tuple-element.204), channel_id=36, replica_groups=mesh['fsdp'=32] {'fsdp'}, dimensions={1}, use_global_device_ids=true | all-gather | bytes 633600 | tf_op jit(solution)/shard_map/all_gather | solution.py:119
  1013.9 10.5 convolution_bitcast_fusion
  1024.8 18.7 fusion.18
  1043.4 11.3 fusion.43
  1054.8 13.1 multiply_reduce_fusion
  1070.8 15.1 all-gather.83.cloned.1.call-done
  1097.0 11.0 fusion.127
  1108.3 12.3 fusion.86
  1130.0 18.4 all-gather.85.cloned.1.call-done
  1159.1 56.6 %all-gather.87.cloned.1.call-done = bf16[1,2560,960]{2,1,0:T(8,128)(2,1)} async-done(((bf16[1,80,960]{2,1,0:T(8,128)(2,1)}), bf16[1,2560,960]{2,1,0:T(8,128)(2,1)}) %all-gather.87.cloned.1.call-update) | async-done | bytes 4915216 | tf_op jit(solution)/shard_map/all_gather | solution.py:119
  1215.7 18.0 multiply_convert_fusion.1
  1233.6 67.2 %all-gather.91.cloned.1.call-done = bf16[1,960,2560]{2,0,1:T(2,128)(2,1)} async-done(((bf16[1,30,2560]{2,0,1:T(2,128)(2,1)}), bf16[1,960,2560]{2,0,1:T(2,128)(2,1)}) %all-gather.91.cloned.1.call-update) | async-done | bytes 4915216 | tf_op jit(solution)/shard_map/all_gather | solution.py:119
  1300.9 11.3 fusion.37
  1312.2 73.8 %all-gather.89.cloned.1.call-done = bf16[1,960,2560]{2,0,1:T(2,128)(2,1)} async-done(((bf16[1,30,2560]{2,0,1:T(2,128)(2,1)}), bf16[1,960,2560]{2,0,1:T(2,128)(2,1)}) %all-gather.89.cloned.1.call-update) | async-done | bytes 4915216 | tf_op jit(solution)/shard_map/all_gather | solution.py:119
  1386.0 13.1 multiply_reduce_fusion.1
  1402.2 47.2 %all-gather.93.cloned.1.call-done = bf16[1,960,960]{2,0,1:T(2,128)(2,1)} async-done(((bf16[1,30,960]{2,0,1:T(2,128)(2,1)}), bf16[1,960,960]{2,0,1:T(2,128)(2,1)}) %all-gather.93.cloned.1.call-update) | async-done | bytes 1843216 | tf_op jit(solution)/shard_map/all_gather | solution.py:119
  1460.4 11.4 fusion.128
  1472.9 12.5 fusion.84
  1489.1 10.9 convolution_bitcast_fusion.1
  1546.9 648.5 %fusion.173 = (f32[32,960]{1,0:T(8,128)S(1)}, f32[32,960]{1,0:T(8,128)S(1)}, f32[32,320]{1,0:T(8,128)}, f32[32,320]{1,0:T(8,128)}, f32[32,320]{1,0:T(8,128)}, /*...) fusion(f32[960,960]{1,0:T(8,128)} %convolution_bitcast_fusion.8, ...), kind=kCustom, calls=%all-reduce-scatter.12 | all-reduce-scatter fusion | flops 10485761 | bytes 40632320
  2233.5 40.4 %all-reduce.36 = (f32[960]{0:T(1024)S(1)}, f32[960]{0:T(1024)S(1)}, f32[960]{0:T(1024)S(1)}, f32[960]{0:T(1024)S(1)}) all-reduce(f32[960]{0:T(1024)S(1)} %copy-done.78, f32[960]{0:T(1024)} %get-tuple-element.124, f32[960]{0:T(1024)} %get-tuple-element.122, f32[960]{0:T(1024)} %get-tuple-element.120), channel_id=53, replica_groups=mesh['fsdp'=32] {'fsdp'}, use_global_device_ids=true, to_apply=%region_31.32.clone | all-reduce | flops 3840 | bytes 30720
  2280.4 9.6 convolution_bitcast_fusion.3
  2297.7 229.4 %fusion.174 = (f32[32,2560]{1,0:T(8,128)S(1)}, f32[32,2560]{1,0:T(8,128)S(1)}) fusion(f32[960,2560]{1,0:T(8,128)} %convolution_bitcast_fusion.2, f32[960,2560]{1,0:T(8,128)} %convolution_bitcast_fusion.3), kind=kCustom, calls=%all-reduce-scatter.13 | all-reduce-scatter fusion | flops 5242881 | bytes 20316160
  (484 shorter events, 362.2 us)
Async XLA Ops:
  7.2 256.8 %all-gather.57.cloned.1.call-start = ((), (), s32[]{:S(2)}) async-start(), calls=%async_computation.4 | async-start | bytes 4055040 | tf_op jit(solution)/shard_map/all_gather | solution.py:119
  9.3 280.3 %all-gather.59.cloned.1.call-start = ((), (), s32[]{:S(2)}) async-start(), calls=%async_computation.5 | async-start | bytes 4055040 | tf_op jit(solution)/shard_map/all_gather | solution.py:119
  11.3 295.2 %all-gather.67.cloned.1.call-start = ((), (), s32[]{:S(2)}) async-start(), calls=%async_computation.9 | async-start | bytes 4055040 | tf_op jit(solution)/shard_map/all_gather | solution.py:119
  12.0 305.2 %all-gather.69.cloned.1.call-start = ((), (), s32[]{:S(2)}) async-start(), calls=%async_computation.10 | async-start | bytes 4055040 | tf_op jit(solution)/shard_map/all_gather | solution.py:119
  12.6 347.4 %all-gather.61.cloned.1.call-start = ((), (), s32[]{:S(2)}) async-start(), calls=%async_computation.6 | async-start | bytes 10137600 | tf_op jit(solution)/shard_map/all_gather | solution.py:119
  15.2 429.9 %all-gather.63.cloned.1.call-start = ((), (), s32[]{:S(2)}) async-start(), calls=%async_computation.7 | async-start | bytes 10137600 | tf_op jit(solution)/shard_map/all_gather | solution.py:119
  16.8 496.4 %all-gather.65.cloned.1.call-start = ((), (), s32[]{:S(2)}) async-start(), calls=%async_computation.8 | async-start | bytes 5406720 | tf_op jit(solution)/shard_map/all_gather | solution.py:119
  17.7 580.9 %all-gather.71.cloned.1.call-start = ((), (), s32[]{:S(2)}) async-start(), calls=%async_computation.11 | async-start | bytes 10137600 | tf_op jit(solution)/shard_map/all_gather | solution.py:119
  18.4 665.4 %all-gather.73.cloned.1.call-start = ((), (), s32[]{:S(2)}) async-start(), calls=%async_computation.12 | async-start | bytes 10137600 | tf_op jit(solution)/shard_map/all_gather | solution.py:119
  19.2 732.7 %all-gather.75.cloned.1.call-start = ((), (), s32[]{:S(2)}) async-start(), calls=%async_computation.13 | async-start | bytes 5406720 | tf_op jit(solution)/shard_map/all_gather | solution.py:119
  19.7 1005.0 %all-gather.77.cloned.1.call-start = ((), (), s32[]{:S(2)}) async-start(), calls=%async_computation.14 | async-start | bytes 5406720 | tf_op jit(solution)/shard_map/all_gather | solution.py:119
  762.9 280.6 %all-gather.81.cloned.1.call-start = ((), (), s32[]{:S(2)}) async-start(), calls=%async_computation.16 | async-start | bytes 10137600 | tf_op jit(solution)/shard_map/all_gather | solution.py:119
  764.4 290.3 %all-gather.79.cloned.1.call-start = ((), (), s32[]{:S(2)}) async-start(), calls=%async_computation.15 | async-start | bytes 10137600 | tf_op jit(solution)/shard_map/all_gather | solution.py:119
  766.0 319.9 %all-gather.83.cloned.1.call-start = ((), (), s32[]{:S(2)}) async-start(), calls=%async_computation.17 | async-start | bytes 4055040 | tf_op jit(solution)/shard_map/all_gather | solution.py:119
  767.0 381.4 %all-gather.85.cloned.1.call-start = ((), (), s32[]{:S(2)}) async-start(), calls=%async_computation.18 | async-start | bytes 4055040 | tf_op jit(solution)/shard_map/all_gather | solution.py:119
  768.1 447.6 %all-gather.87.cloned.1.call-start = ((), (), s32[]{:S(2)}) async-start(), calls=%async_computation.19 | async-start | bytes 5406720 | tf_op jit(solution)/shard_map/all_gather | solution.py:119
  768.6 532.2 %all-gather.91.cloned.1.call-start = ((), (), s32[]{:S(2)}) async-start(), calls=%async_computation.21 | async-start | bytes 10137600 | tf_op jit(solution)/shard_map/all_gather | solution.py:119
  769.2 616.8 %all-gather.89.cloned.1.call-start = ((), (), s32[]{:S(2)}) async-start(), calls=%async_computation.20 | async-start | bytes 10137600 | tf_op jit(solution)/shard_map/all_gather | solution.py:119
  769.8 679.5 %all-gather.93.cloned.1.call-start = ((), (), s32[]{:S(2)}) async-start(), calls=%async_computation.22 | async-start | bytes 4055040 | tf_op jit(solution)/shard_map/all_gather | solution.py:119
  770.6 1453.3 %all-gather.95.cloned.1.call-start = ((), (), s32[]{:S(2)}) async-start(), calls=%async_computation.23 | async-start | bytes 4055040 | tf_op jit(solution)/shard_map/all_gather | solution.py:119
  811.2 1818.5 %reduce-scatter.29.cloned.1.call-start = ((), (), s32[]{:S(2)}) async-start(), calls=%async_computation.3 | async-start | bytes 10813440 | tf_op jit(solution)/shard_map/reduce_scatter | solution.py:136
  1024.5 1605.2 %reduce-scatter.27.cloned.1.call-start = ((), (), s32[]{:S(2)}) async-start(), calls=%async_computation.2 | async-start | bytes 10813440 | tf_op jit(solution)/shard_map/reduce_scatter | solution.py:136
  1546.9 673.9 %copy-start.29 = (bf16[1,960,320]{1,2,0:T(8,128)(2,1)S(1)}, bf16[1,960,320]{1,2,0:T(8,128)(2,1)}, u32[]{:S(2)}) copy-start(bf16[1,960,320]{1,2,0:T(8,128)(2,1)} %copy.110) | copy-start | bytes 1843204
  1546.9 673.9 %copy-start.34 = (bf16[8,128,5,64]{1,3,2,0:T(8,128)(2,1)S(1)}, bf16[8,128,5,64]{1,3,2,0:T(8,128)(2,1)}, u32[]{:S(2)}) copy-start(bf16[8,128,5,64]{1,3,2,0:T(8,128)(2,1)} %copy-done.33) | copy-start | bytes 1966084
  2196.7 337.0 %collective-permute-start.8 = (f32[32,320]{1,0:T(8,128)}, f32[32,320]{1,0:T(8,128)}, u32[]{:S(2)}, u32[]{:S(2)}) collective-permute-start(f32[32,320]{1,0:T(8,128)} %get-tuple-element.155), channel_id=1, source_target_pairs={{0,1},{1,2},{2,3},{3,4},{4,5},{5,6},{6,7},{7,8},{8,9},{9,10},{10,1... | collective-permute-start | bytes 122888
  2202.6 339.9 %collective-permute-start.10 = (f32[32,320]{1,0:T(8,128)}, f32[32,320]{1,0:T(8,128)}, u32[]{:S(2)}, u32[]{:S(2)}) collective-permute-start(f32[32,320]{1,0:T(8,128)} %get-tuple-element.154), channel_id=1, source_target_pairs={{0,1},{1,2},{2,3},{3,4},{4,5},{5,6},{6,7},{7,8},{8,9},{9,10},{10,1... | collective-permute-start | bytes 122888
  2207.3 320.7 %collective-permute-start.9 = (f32[30,320]{1,0:T(8,128)}, f32[30,320]{1,0:T(8,128)}, u32[]{:S(2)}, u32[]{:S(2)}) collective-permute-start(f32[30,320]{1,0:T(8,128)} %slice.292), channel_id=1, source_target_pairs={{0,2},{1,3},{2,4},{3,5},{4,6},{5,7},{6,8},{7,9},{8,10},{9,11},{10,... | collective-permute-start | bytes 115208
  2214.7 317.8 %collective-permute-start.11 = (f32[30,320]{1,0:T(8,128)}, f32[30,320]{1,0:T(8,128)}, u32[]{:S(2)}, u32[]{:S(2)}) collective-permute-start(f32[30,320]{1,0:T(8,128)} %slice.293), channel_id=1, source_target_pairs={{0,2},{1,3},{2,4},{3,5},{4,6},{5,7},{6,8},{7,9},{8,10},{9,11},{10,... | collective-permute-start | bytes 115208
  2218.7 330.8 %collective-permute-start.4 = (f32[32,320]{1,0:T(8,128)}, f32[32,320]{1,0:T(8,128)}, u32[]{:S(2)}, u32[]{:S(2)}) collective-permute-start(f32[32,320]{1,0:T(8,128)} %get-tuple-element.153), channel_id=1, source_target_pairs={{0,1},{1,2},{2,3},{3,4},{4,5},{5,6},{6,7},{7,8},{8,9},{9,10},{10,1... | collective-permute-start | bytes 122888
  2528.0 27.5 %collective-permute-start.6 = (f32[32,320]{1,0:T(8,128)S(1)}, f32[32,320]{1,0:T(8,128)S(1)}, u32[]{:S(2)}, u32[]{:S(2)}) collective-permute-start(f32[32,320]{1,0:T(8,128)S(1)} %copy-done.68), channel_id=1, source_target_pairs={{0,1},{1,2},{2,3},{3,4},{4,5},{5,6},{6,7},{7,8},{8,9},{9,10},{10,1... | collective-permute-start | bytes 122888
  2532.5 15.1 collective-permute-start.5
  2533.8 19.5 collective-permute-start.7
  2542.5 61.7 %collective-permute-start.20 = (f32[32,2560]{1,0:T(8,128)S(1)}, f32[32,2560]{1,0:T(8,128)}, u32[]{:S(2)}, u32[]{:S(2)}) collective-permute-start(f32[32,2560]{1,0:T(8,128)S(1)} %get-tuple-element.163), channel_id=1, source_target_pairs={{0,1},{1,2},{2,3},{3,4},{4,5},{5,6},{6,7},{7,8},{8,9},{9,10},{10,1... | collective-permute-start | bytes 983048
  2547.5 16.5 collective-permute-start.12
  2549.5 24.6 collective-permute-start.14
  2553.3 7.0 collective-permute-start.13
  2555.6 12.5 collective-permute-start.15
  2560.2 23.3 collective-permute-start
  2564.1 28.0 %collective-permute-start.2 = (f32[32,960]{1,0:T(8,128)S(1)}, f32[32,960]{1,0:T(8,128)}, u32[]{:S(2)}, u32[]{:S(2)}) collective-permute-start(f32[32,960]{1,0:T(8,128)S(1)} %get-tuple-element.150), channel_id=1, source_target_pairs={{0,1},{1,2},{2,3},{3,4},{4,5},{5,6},{6,7},{7,8},{8,9},{9,10},{10,1... | collective-permute-start | bytes 368648
  2568.1 13.1 collective-permute-start.1
  2574.1 13.5 collective-permute-start.3
  2581.2 33.7 %collective-permute-start.22 = (f32[32,2560]{1,0:T(8,128)S(1)}, f32[32,2560]{1,0:T(8,128)}, u32[]{:S(2)}, u32[]{:S(2)}) collective-permute-start(f32[32,2560]{1,0:T(8,128)S(1)} %get-tuple-element.162), channel_id=1, source_target_pairs={{0,1},{1,2},{2,3},{3,4},{4,5},{5,6},{6,7},{7,8},{8,9},{9,10},{10,1... | collective-permute-start | bytes 983048
  2583.6 40.6 %collective-permute-start.16 = (f32[32,2560]{1,0:T(8,128)S(1)}, f32[32,2560]{1,0:T(8,128)}, u32[]{:S(2)}, u32[]{:S(2)}) collective-permute-start(f32[32,2560]{1,0:T(8,128)S(1)} %get-tuple-element.159), channel_id=1, source_target_pairs={{0,1},{1,2},{2,3},{3,4},{4,5},{5,6},{6,7},{7,8},{8,9},{9,10},{10,1... | collective-permute-start | bytes 983048
  2587.6 10.5 collective-permute-start.21
  2592.0 19.4 collective-permute-start.23
  2598.1 28.5 %collective-permute-start.18 = (f32[32,2560]{1,0:T(8,128)S(1)}, f32[32,2560]{1,0:T(8,128)S(1)}, u32[]{:S(2)}, u32[]{:S(2)}) collective-permute-start(f32[32,2560]{1,0:T(8,128)S(1)} %get-tuple-element.158), channel_id=1, source_target_pairs={{0,1},{1,2},{2,3},{3,4},{4,5},{5,6},{6,7},{7,8},{8,9},{9,10},{10,1... | collective-permute-start | bytes 983048
  2604.2 20.0 collective-permute-start.17
  2611.4 15.2 collective-permute-start.19
  (90 other events, 1991.2 us)
Sparse Core Ops, SparseCore 0:
  10.9 64.5 all-gather.56
  78.4 63.1 all-gather.58
  144.5 64.2 all-gather.66
  211.5 63.3 all-gather.68
  278.2 81.6 all-gather.60
  362.7 82.3 all-gather.62
  448.5 64.6 all-gather.64
  516.7 81.8 all-gather.70
  601.5 82.3 all-gather.72
  687.1 64.6 all-gather.74
  763.0 66.7 all-gather.76
  833.0 93.6 all-gather.80
  929.6 92.2 all-gather.78
  1024.7 61.1 all-gather.82
  1088.6 59.7 all-gather.84
  1151.7 63.9 all-gather.86
  1219.0 81.8 all-gather.90
  1303.6 82.3 all-gather.88
  1388.9 60.4 all-gather.92
  1452.1 59.7 all-gather.94
  1514.1 229.4 reduce-scatter.28
  1745.9 244.0 reduce-scatter.26
where the time goes:
time: 2650 us; the launch traced here: 2640 us
  blocking collectives  1360 us (51%)
  waiting for transfers between devices  621 us (23%)
  matrix products  359 us (14%)
  local copies, waits for them, and re-layouts  139 us (5%)
  starting transfers between devices  84.5 us (3%)
  other arithmetic  55.3 us (2%)
    unnamed x5, blocking collectives  1000 us
    all_gather x20, waiting for transfers between devices, gather_layer(): lax.all_gather(master[layer_idx].astype(jnp.bfloat16), 'fsdp', axis=0, ti...  616 us
    all_gather x8, blocking collectives, gather_layer(): lax.all_gather(master[layer_idx].astype(jnp.bfloat16), 'fsdp', axis=0, ti...  364 us
    unnamed x24, starting transfers between devices  83.3 us
    all_gather x12, local copies, waits for them, and re-layouts, gather_layer(): lax.all_gather(master[layer_idx].astype(jnp.bfloat16), 'fsdp', axis=0, ti...  69.5 us
    unnamed x234, local copies, waits for them, and re-layouts  56.3 us
  transfers between devices with their start and end apart: 46, of which 12 were waited for; matrix products, arithmetic and copies ran while one was open for 53% of the time, Pallas kernels for 0%

commit v1 on v0

v1 whole, which is shorter than its diff:
```python
import jax
import jax.numpy as jnp
from jax import lax
from jax.experimental import pallas as pl
from jax.experimental.pallas import tpu as pltpu
from jax.sharding import PartitionSpec as P

NORM_EPS = 1e-5
MASK_VALUE = -1e30
BF = jnp.bfloat16
F32 = jnp.float32
DEVICES = 32
DIM = 960
ROWS = 30
PAD_ROWS = 32
PAD_DIM = DEVICES * PAD_ROWS
FFN_ROWS = 80
QKV = 1600
QKV_PAD = 1664


def flip(bits):
    return [(i, i ^ bits) for i in range(DEVICES)]


CORE, XAX, YAX = 1, 2, 4


def send(values, bits):
    return lax.ppermute(values, "fsdp", flip(bits))


def block_of(dev):
    core, x_at, y_at, z_at = dev % 2, dev // 2 % 2, dev // 4 % 2, dev // 8
    return ((core * 2 + x_at) * 2 + y_at) * 4 + z_at


def one_hot(target, width):
    return (target[:, None] == lax.broadcasted_iota(jnp.int32, (target.shape[0], width), 1)).astype(BF)


def swap_xy(block):
    return (block & 19) | ((block & 8) >> 1) | ((block & 4) << 1)


def dot(left, right, dims):
    return lax.dot_general(left, right, ((dims[:1], dims[1:]), ((), ())), preferred_element_type=F32)


def mm(left, right):
    return dot(left, right, (1, 0))


def pick(values, index):
    return lax.dynamic_index_in_dim(values, index, 0, keepdims=False)


def rms_forward(values, gain):
    vals32 = values.astype(F32)
    inv_rms = lax.rsqrt(jnp.sum(vals32 * vals32, axis=-1, keepdims=True) * (1.0 / DIM) + NORM_EPS)
    return (vals32 * inv_rms * gain.astype(F32)).astype(BF), inv_rms


def rms_backward(values, inv_rms, gain, grad_normed):
    scaled = values.astype(F32) * inv_rms
    grad_scaled = grad_normed * gain.astype(F32)
    grad_gain = jnp.sum(grad_normed * scaled, axis=0)
    mean = jnp.sum(grad_scaled * scaled, axis=-1, keepdims=True) * (1.0 / DIM)
    return inv_rms * (grad_scaled - scaled * mean), grad_gain


def rotary(heads32, rope_cos, rope_sin, sin_sign):
    half_dim = rope_cos.shape[-1]
    first_half = heads32[..., :half_dim]
    second_half = heads32[..., half_dim:]
    cos_b = rope_cos[None, :, None, :]
    sin_b = sin_sign * rope_sin[None, :, None, :]
    return jnp.concatenate([first_half * cos_b - second_half * sin_b, second_half * cos_b + first_half * sin_b], axis=-1)


def layer_forward(weights, rope_cos, rope_sin, hidden, batch, seq_len):
    w_qkv, w_out, w_gate, w_up, w_down, gain_attn, gain_mlp = weights
    head_dim = 2 * rope_cos.shape[-1]
    num_heads, kv_heads = 15, 5
    normed, inv_attn = rms_forward(hidden, gain_attn)
    qkv = mm(normed, w_qkv)
    q_heads = rotary(qkv[:, :960].reshape(batch, seq_len, num_heads, head_dim), rope_cos, rope_sin, 1.0).astype(BF)
    q_heads = q_heads.reshape(batch, seq_len, kv_heads, 3, head_dim)
    k_heads = rotary(qkv[:, 960:1280].reshape(batch, seq_len, kv_heads, head_dim), rope_cos, rope_sin, 1.0).astype(BF)
    v_heads = qkv[:, 1280:1600].astype(BF).reshape(batch, seq_len, kv_heads, head_dim)
    scores = jnp.einsum("bqkgd,bskd->bkgqs", q_heads, k_heads, preferred_element_type=F32) * head_dim ** -0.5
    positions = jnp.arange(seq_len)
    scores = jnp.where(positions[:, None] >= positions[None, :], scores, MASK_VALUE)
    probs = jax.nn.softmax(scores, axis=-1).astype(BF)
    heads = jnp.einsum("bkgqs,bskd->bqkgd", probs, v_heads, preferred_element_type=F32)
    heads = heads.astype(BF).reshape(batch * seq_len, num_heads * head_dim)
    mid = (hidden.astype(F32) + mm(heads, w_out)).astype(BF)
    normed_mlp, inv_mlp = rms_forward(mid, gain_mlp)
    gate_pre = mm(normed_mlp, w_gate)
    up_proj = mm(normed_mlp, w_up)
    act = (jax.nn.silu(gate_pre) * up_proj).astype(BF)
    out = (mid.astype(F32) + mm(act, w_down)).astype(BF)
    return out, (hidden, inv_attn, normed, q_heads, k_heads, v_heads, probs, heads, mid, inv_mlp, normed_mlp, gate_pre, up_proj, act)


def scatter_wide(left_rel, grad, first, second, extra=None):
    def piece(at):
        rows = slice(at * 256, (at + 1) * 256)
        part = dot(left_rel[:, rows], grad, (0, 0))
        return part if extra is None else part + extra[rows]

    far = send(piece(3), CORE)
    near = send(piece(2), CORE)
    across = send(piece(1) + far, first)
    kept = piece(0) + near + across
    return kept[:128] + send(kept[128:], second)


def scatter_down(act, grad, place):
    core, x_at, y_at, z_at = place
    whole = dot(act, grad, (0, 0)).reshape(4, 640, PAD_DIM)

    def piece(d_core, d_x):
        return pick(whole, (core ^ d_core) * 2 + (x_at ^ d_x))

    far = send(piece(1, 1), CORE)
    near = send(piece(1, 0), CORE)
    across = send(piece(0, 1) + far, XAX)
    kept = (piece(0, 0) + near + across).reshape(2, 4 * FFN_ROWS, PAD_DIM)
    part = pick(kept, y_at) + send(pick(kept, y_at ^ 1), YAX)
    part = part.reshape(4, FFN_ROWS, PAD_DIM)
    return jnp.concatenate([pick(part, z_at ^ step) for step in range(4)])


def scatter_z(part):
    half = part.shape[0] // 2
    part = part[:half] + send(part[half:], 16)
    half = half // 2
    return part[:half] + send(part[half:], 8)


def layer_backward(weights, rope_cos, rope_sin, saved, grad_out, batch, seq_len, place, to_rel, nat_to_rel):
    w_qkv, w_out, w_gate, w_up, w_down, gain_attn, gain_mlp = weights
    (hidden, inv_attn, normed, q_heads, k_heads, v_heads, probs, heads, mid, inv_mlp, normed_mlp, gate_pre, up_proj, act) = saved
    head_dim = 2 * rope_cos.shape[-1]
    num_heads = 15
    tokens = hidden.shape[0]
    rel_x, rel_y = to_rel
    down = scatter_down(act, grad_out, place)
    grad_act = dot(grad_out, w_down, (1, 1))
    gate_sig = jax.nn.sigmoid(gate_pre)
    grad_up = (grad_act * gate_pre * gate_sig).astype(BF)
    grad_gate = (grad_act * up_proj * gate_sig * (1.0 + gate_pre * (1.0 - gate_sig))).astype(BF)
    gate = scatter_wide(mm(normed_mlp, rel_x).astype(BF), grad_gate, XAX, YAX)
    up = scatter_wide(mm(normed_mlp, rel_y).astype(BF), grad_up, YAX, XAX)
    from_gate = dot(grad_gate, w_gate, (1, 1))
    grad_normed_mlp = from_gate + dot(grad_up, w_up, (1, 1))
    grad_mid_norm, grad_gain_mlp = rms_backward(mid, inv_mlp, gain_mlp, grad_normed_mlp)
    grad_mid = grad_out.astype(F32) + grad_mid_norm
    grad_mid_bf = grad_mid.astype(BF)
    out = scatter_wide(mm(heads, nat_to_rel).astype(BF), grad_mid_bf, YAX, XAX)
    grad_attn = dot(grad_mid_bf, w_out, (1, 1)).astype(BF).reshape(batch, seq_len, 5, 3, head_dim)
    grad_v = jnp.einsum("bkgqs,bqkgd->bskd", probs, grad_attn, preferred_element_type=F32)
    grad_v = grad_v.astype(BF).reshape(tokens, -1)
    grad_probs = jnp.einsum("bqkgd,bskd->bkgqs", grad_attn, v_heads, preferred_element_type=F32)
    probs32 = probs.astype(F32)
    grad_scores = probs32 * (grad_probs - jnp.sum(probs32 * grad_probs, axis=-1, keepdims=True)) * head_dim ** -0.5
    grad_scores = grad_scores.astype(BF)
    grad_q = jnp.einsum("bkgqs,bskd->bqkgd", grad_scores, k_heads, preferred_element_type=F32)
    grad_q = rotary(grad_q.reshape(batch, seq_len, num_heads, head_dim), rope_cos, rope_sin, -1.0)
    grad_q = grad_q.astype(BF).reshape(tokens, -1)
    grad_k = jnp.einsum("bkgqs,bqkgd->bskd", grad_scores, q_heads, preferred_element_type=F32)
    grad_k = rotary(grad_k, rope_cos, rope_sin, -1.0).astype(BF).reshape(tokens, -1)
    grad_qkv = jnp.concatenate([grad_q, grad_k, grad_v, jnp.zeros((tokens, QKV_PAD - QKV), BF)], axis=1)
    grad_normed = dot(grad_qkv, w_qkv, (1, 1))
    grad_hidden_norm, grad_gain_attn = rms_backward(hidden, inv_attn, gain_attn, grad_normed)
    grad_hidden = (grad_mid + grad_hidden_norm).astype(BF)
    gains = jnp.stack([grad_gain_attn, grad_gain_mlp])
    gain_rows = lax.dot_general(rel_y.astype(F32), gains, (((0,), (1,)), ((), ())), precision=lax.Precision.HIGHEST, preferred_element_type=F32)
    extra = jnp.pad(gain_rows, ((0, 0), (QKV, QKV_PAD - QKV - 2)))
    qkv = scatter_wide(mm(normed, rel_y).astype(BF), grad_qkv, YAX, XAX, extra)
    down = scatter_z(down)
    mlp = scatter_z(jnp.concatenate([gate, up], axis=1))
    attn = scatter_z(jnp.concatenate([qkv, out], axis=1))
    return grad_hidden, (attn[:, :QKV_PAD], attn[:, QKV_PAD:], mlp[:, :2560], mlp[:, 2560:], down)


def gather_kernel(*refs):
    count = (len(refs) - 3) // 2
    shards, wholes = refs[:count], refs[count:2 * count]
    send_sem, recv_sem, own_sem = refs[2 * count:]
    me = lax.axis_index("fsdp")
    core, x_at, y_at, z_at = me % 2, me // 2 % 2, me // 4 % 2, me // 8
    core_peer = me + 1 - 2 * core
    x_peer = me + 2 - 4 * x_at
    y_peer = me + 4 - 8 * y_at
    z_peers = [(z_at + step) % 4 * 8 + me % 8 for step in (1, 2, 3)]
    barrier = pltpu.get_barrier_semaphore()
    for peer in (core_peer, x_peer, y_peer, *z_peers):
        pl.semaphore_signal(barrier, inc=1, device_id=(peer,), device_id_type=pl.DeviceIdType.MESH)
    pl.semaphore_wait(barrier, 6)

    def copy(index, stage, source, target, peer):
        return pltpu.make_async_remote_copy(src_ref=source, dst_ref=target, send_sem=send_sem.at[index, stage], recv_sem=recv_sem.at[index, stage],
                                            device_id=(peer,), device_id_type=pl.DeviceIdType.MESH)

    def z_copies(index):
        return [copy(index, step, shards[index], wholes[index].at[core, x_at, y_at, z_at], z_peers[step]) for step in range(3)]

    def second(index):
        part = wholes[index].at[core, x_at, y_at]
        return copy(index, 3, part, part, y_peer if index % 5 in (2, 4) else x_peer)

    def third(index):
        if index % 5 in (2, 4):
            part = wholes[index].at[core, x_at]
            return copy(index, 4, part, part, x_peer)
        part = wholes[index].at[core, :, y_at]
        return copy(index, 4, part, part, y_peer)

    def last(index):
        part = wholes[index].at[core]
        return copy(index, 5, part, part, core_peer)

    def own(index):
        return pltpu.make_async_copy(shards[index], wholes[index].at[core, x_at, y_at, z_at], own_sem.at[index])

    for index in range(count):
        own(index).start()
        for one in z_copies(index):
            one.start()
    for index in range(count):
        own(index).wait()
        for one in z_copies(index):
            one.wait()
        second(index).start()
        if index >= 2:
            second(index - 2).wait()
            third(index - 2).start()
        if index >= 5:
            third(index - 5).wait()
            last(index - 5).start()
    for index in (count - 2, count - 1):
        second(index).wait()
        third(index).start()
    for index in range(count - 5, count):
        third(index).wait()
        last(index).start()
    for index in range(count):
        last(index).wait()


def gather_all(shards):
    count = len(shards)
    wholes = pl.pallas_call(
        gather_kernel,
        out_shape=[jax.ShapeDtypeStruct((2, 2, 2, 4) + shard.shape, BF) for shard in shards],
        in_specs=[pl.BlockSpec(memory_space=pltpu.VMEM)] * count,
        out_specs=[pl.BlockSpec(memory_space=pl.ANY)] * count,
        scratch_shapes=[pltpu.SemaphoreType.DMA((count, 6)), pltpu.SemaphoreType.DMA((count, 6)), pltpu.SemaphoreType.DMA((count,))],
        compiler_params=pltpu.CompilerParams(collective_id=0, has_side_effects=True, vmem_limit_bytes=8 * 1024 * 1024),
    )(*shards)
    return [whole.reshape(DEVICES * whole.shape[4], whole.shape[5]) for whole in wholes]


def solution(mesh):
    shard_spec = P(None, "fsdp")
    batch_spec = P("fsdp")

    def local_step(w_query, w_key, w_value, w_out, w_gate, w_up, w_down, gain_attn, gain_mlp, rope_cos, rope_sin, x_in, y_cot):
        me = lax.axis_index("fsdp")
        place = (me % 2, me // 2 % 2, me // 4 % 2, me // 8)
        my_block = block_of(me)
        batch, seq_len, _ = x_in.shape
        tokens = batch * seq_len
        natural = lax.iota(jnp.int32, DIM)
        nat_block, nat_row = block_of(natural // ROWS), natural % ROWS
        spread = one_hot(nat_block * PAD_ROWS + nat_row, PAD_DIM)
        nat_to_rel = one_hot(swap_xy(nat_block ^ my_block) * PAD_ROWS + nat_row, PAD_DIM)
        padded = lax.iota(jnp.int32, PAD_DIM)
        rel_block = (padded // PAD_ROWS) ^ my_block
        rel_x = one_hot(rel_block * PAD_ROWS + padded % PAD_ROWS, PAD_DIM)
        rel_y = one_hot(swap_xy(rel_block) * PAD_ROWS + padded % PAD_ROWS, PAD_DIM)

        def pad_rows(values):
            return jnp.pad(values, ((0, 0), (0, PAD_ROWS - ROWS), (0, 0)))

        def ffn_columns(values):
            return values.reshape(2, ROWS, 4, 2, 2, 2, FFN_ROWS).transpose(0, 1, 5, 4, 3, 2, 6).reshape(2, ROWS, -1)

        sh_qkv = pad_rows(jnp.concatenate([w_query, w_key, w_value, gain_attn[:, :, None], gain_mlp[:, :, None], jnp.zeros((2, ROWS, QKV_PAD - QKV - 2), F32)], axis=2).astype(BF))
        sh_out = pad_rows(mm(w_out.astype(BF).reshape(2 * ROWS, DIM), spread).astype(BF).reshape(2, ROWS, PAD_DIM))
        sh_gate = pad_rows(ffn_columns(w_gate.astype(BF)))
        sh_up = pad_rows(ffn_columns(w_up.astype(BF)))
        sh_down = mm(w_down.astype(BF).reshape(2 * FFN_ROWS, DIM), spread).astype(BF).reshape(2, FFN_ROWS, PAD_DIM)

        hidden = mm(x_in.reshape(tokens, DIM), spread).astype(BF)
        grad_hidden = mm(y_cot.reshape(tokens, DIM), spread).astype(BF)
        saved_layers, layer_weights = [], []
        wholes = gather_all([part[layer] for layer in range(2) for part in (sh_qkv, sh_out, sh_gate, sh_up, sh_down)])
        for layer in range(2):
            full_qkv, full_out, full_gate, full_up, full_down = wholes[5 * layer:5 * layer + 5]
            full_out = mm(spread, full_out).astype(BF)
            weights = (full_qkv, full_out, full_gate, full_up, full_down, full_qkv[:, QKV], full_qkv[:, QKV + 1])
            hidden, saved = layer_forward(weights, rope_cos, rope_sin, hidden, batch, seq_len)
            saved_layers.append(saved)
            layer_weights.append(weights)
        y_out = dot(hidden, spread, (1, 1)).astype(BF).reshape(x_in.shape)
        shards = [None, None]
        for layer in (1, 0):
            grad_hidden, shards[layer] = layer_backward(layer_weights[layer], rope_cos, rope_sin, saved_layers[layer], grad_hidden, batch, seq_len, place, (rel_x, rel_y), nat_to_rel)
        dx_in = dot(grad_hidden, spread, (1, 1)).astype(BF).reshape(x_in.shape)

        g_qkv, g_out, g_gate, g_up, g_down = (jnp.stack(pair) for pair in zip(*shards))

        def natural_columns(values, rows):
            flat = values.reshape(2 * values.shape[1], PAD_DIM)
            flat = lax.dot_general(flat, spread.astype(F32), (((1,), (1,)), ((), ())), precision=lax.Precision.HIGHEST, preferred_element_type=F32)
            return flat.reshape(2, values.shape[1], DIM)[:, :rows]

        def natural_ffn(values):
            return values[:, :ROWS].reshape(2, ROWS, 2, 2, 2, 4, FFN_ROWS).transpose(0, 1, 5, 4, 3, 2, 6).reshape(2, ROWS, -1)

        g_qkv = g_qkv[:, :ROWS]
        return (y_out, dx_in, g_qkv[:, :, :960], g_qkv[:, :, 960:1280], g_qkv[:, :, 1280:1600], natural_columns(g_out, ROWS),
                natural_ffn(g_gate), natural_ffn(g_up), natural_columns(g_down, FFN_ROWS), g_qkv[:, :, QKV], g_qkv[:, :, QKV + 1])

    in_specs = (shard_spec,) * 9 + (P(), P(), batch_spec, batch_spec)
    out_specs = (batch_spec, batch_spec) + (shard_spec,) * 9
    return jax.shard_map(local_step, mesh=mesh, in_specs=in_specs, out_specs=out_specs, check_vma=False)
```

time: 2650 us -> 1400 us (0.53)
  blocking collectives: 1360 us -> 0 us
  Pallas kernels: 0 us -> 229 us
  waiting for transfers between devices: 621 us -> 403 us
  matrix products: 359 us -> 441 us
  starting transfers between devices: 84.5 us -> 135 us
    unnamed x5 -> x0, blocking collectives: 1000 us -> none
    all_gather x20 -> x0, waiting for transfers between devices: 616 us -> none  [gather_layer(): lax.all_gather(master[layer_idx].astype(jnp.bfloat16), 'fsdp', axis=0, ti...]
    ppermute x0 -> x52, waiting for transfers between devices: none -> 403 us  [send(): return lax.ppermute(values, 'fsdp', flip(bits))]
    all_gather x8 -> x0, blocking collectives: 364 us -> none  [gather_layer(): lax.all_gather(master[layer_idx].astype(jnp.bfloat16), 'fsdp', axis=0, ti...]
    pallas_call x0 -> x1, Pallas kernels: none -> 229 us  [gather_all(): pl.pallas_call(gather_kernel, out_shape=[jax.ShapeDtypeStruct((2, 2, 2, 4...]
    ppermute x0 -> x52, starting transfers between devices: none -> 135 us  [send(): return lax.ppermute(values, 'fsdp', flip(bits))]
    unnamed x24 -> x0, starting transfers between devices: 83.3 us -> none
    dot_general x46 -> x77, matrix products: 300 us -> 381 us  [the longest x69 360 us: dot(): lax.dot_general(left, right, ((dims[:1], dims[1:]), ((), ())), preferred_...]
  transfers between devices with their start and end apart: 46 -> 52, of which waited for: 12 -> 20; matrix products, arithmetic and copies ran while one was open for 53% -> 23% of each run, Pallas kernels for 0% -> 0%
where the time goes in v1:
time: 1400 us; the launch traced here: 1390 us
  matrix products  441 us (32%)
  waiting for transfers between devices  403 us (29%)
  Pallas kernels  229 us (16%)
  starting transfers between devices  135 us (10%)
  local copies, waits for them, and re-layouts  121 us (9%)
  other arithmetic  60.9 us (4%)
    ppermute x52, waiting for transfers between devices, send(): return lax.ppermute(values, 'fsdp', flip(bits))  403 us
    dot_general x69, matrix products, dot(): lax.dot_general(left, right, ((dims[:1], dims[1:]), ((), ())), preferred_...  360 us
    pallas_call x1, Pallas kernels, gather_all(): pl.pallas_call(gather_kernel, out_shape=[jax.ShapeDtypeStruct((2, 2, 2, 4...  229 us
    ppermute x52, starting transfers between devices, send(): return lax.ppermute(values, 'fsdp', flip(bits))  135 us
    unnamed x374, local copies, waits for them, and re-layouts  47 us
  transfers between devices with their start and end apart: 52, of which 20 were waited for; matrix products, arithmetic and copies ran while one was open for 23% of the time, Pallas kernels for 0%

profile of v1, /device:TPU:1, one launch (start us, length us, event | category | flops | bytes accessed | tf_op | source)
XLA Modules:
  0.0 1394.1 jit_solution(4308613983865975929)
XLA Ops:
  17.0 229.4 %shard_map.212 = (bf16[2,2,2,4,32,1664]{5,4,3,2,1,0:T(8,128)(2,1)S(1)}, bf16[2,2,2,4,32,1024]{5,4,3,2,1,0:T(8,128)(2,1)S(1)}, bf16[2,2,2,4,32,2560]{5,4,3,2,1,0:...) custom-call(bf16[32,1664]{1,0:T(8,128)(2,1)S(1)} %get-tuple-element., ...), custom_call_target="tpu_custom_call" | custom-call | tf_op jit(solution)/shard_map/pallas_call | solution.py:255
  305.9 11.4 fusion.381
  317.3 13.3 multiply_convert_fusion.5
  330.6 9.8 fusion.39
  384.7 11.3 fusion.373
  396.0 8.8 fusion.375
  407.3 19.4 %multiply_convert_fusion.2 = (bf16[1024,2560]{1,0:T(8,128)(2,1)}, bf16[1024,2560]{1,0:T(8,128)(2,1)}, bf16[1024,2560]{1,0:T(8,128)(2,1)}) fusion(f32[1024,2560]{1,0:T(8,128)} %fusion.375, f32[1024,2560]{1,0:T(8,128)} %fusion.373, bf16[1024,1024]{1,0:T(8,128)(2,1)S(1)} %fusion.148, bf16[2560,1024]{1,0:T(8,128)(2,1)} %bitcast.524), kind=kOutput, calls=%fused_computation.14 | convolution fusion | flops 5410652160 | bytes 44040192 | tf_op jit(solution)/shard_map/dot_general | solution.py:47
  426.7 9.3 fusion.392
  436.0 8.5 fusion.46
  456.1 12.2 fusion.97
  468.3 11.9 fusion.191
  521.7 18.3 %multiply_convert_fusion = (bf16[1024,2560]{1,0:T(8,128)(2,1)}, bf16[1024,2560]{1,0:T(8,128)(2,1)}) fusion(f32[1024,2560]{1,0:T(8,128)} %fusion.381, f32[1024,2560]{1,0:T(8,128)} %get-tuple-element.153, bf16[1024,1024]{0,1:T(8,128)(2,1)} %fusion.37, bf16[2560,1024]{1,0:T(8,128)(2,1)} %bitcast.534), kind=kOutput, calls=%fused_computation.12 | convolution fusion | flops 5402787840 | bytes 38797312 | tf_op jit(solution)/shard_map/dot_general | solution.py:47
  540.0 9.7 fusion.393
  574.7 12.7 fusion.95
  587.4 12.2 fusion.192
  615.3 6.4 fusion.59
  629.8 8.6 fusion.394
  660.0 8.4 fusion.395
  668.5 13.3 convert_bitcast_fusion.3
  687.7 9.7 convert_bitcast_fusion
  739.0 7.4 fusion.105
  746.4 9.4 collective-permute-done.16
  757.5 7.6 fusion.103
  765.0 13.2 collective-permute-done.6
  822.0 12.7 collective-permute-done.12
  849.7 21.5 %collective-permute-done.2 = f32[256,1664]{1,0:T(8,128)} collective-permute-done((f32[256,1664]{1,0:T(8,128)}, f32[256,1664]{1,0:T(8,128)}, u32[]{:S(2)}, u32[]{:S(2)}) %collective-permute-start.2) | collective-permute-done | bytes 1703968 | tf_op jit(solution)/shard_map/ppermute | solution.py:30
  882.0 64.8 %collective-permute-done.3 = f32[128,1664]{1,0:T(8,128)S(1)} collective-permute-done((f32[128,1664]{1,0:T(8,128)S(1)}, f32[128,1664]{1,0:T(8,128)S(1)}, u32[]{:S(2)}, u32[]{:S(2)}) %collective-permute-start.3) | collective-permute-done | bytes 852000 | tf_op jit(solution)/shard_map/ppermute | solution.py:30
  946.8 9.8 collective-permute-start.18
  956.8 27.4 %collective-permute-done.18 = f32[64,2688]{1,0:T(8,128)S(1)} collective-permute-done((f32[64,2688]{1,0:T(8,128)S(1)}, f32[64,2688]{1,0:T(8,128)S(1)}, u32[]{:S(2)}, u32[]{:S(2)}) %collective-permute-start.18) | collective-permute-done | bytes 688160 | tf_op jit(solution)/shard_map/ppermute | solution.py:30
  987.9 10.5 collective-permute-done.8
  1022.6 36.7 %collective-permute-done.42 = f32[640,1024]{1,0:T(8,128)} collective-permute-done((f32[640,1024]{1,0:T(8,128)}, f32[640,1024]{1,0:T(8,128)}, u32[]{:S(2)}, u32[]{:S(2)}) %collective-permute-start.42) | collective-permute-done | bytes 2621472 | tf_op jit(solution)/shard_map/ppermute | solution.py:30
  1059.3 18.6 %collective-permute-start.19 = (f32[32,2688]{1,0:T(8,128)}, f32[32,2688]{1,0:T(8,128)S(1)}, u32[]{:S(2)}, u32[]{:S(2)}) collective-permute-start(f32[32,2688]{1,0:T(8,128)} %slice.591), channel_id=1, source_target_pairs={{0,8},{1,9},{2,10},{3,11},{4,12},{5,13},{6,14},{7,15},{8,0},{9,1},... | collective-permute-start | bytes 1032200 | tf_op jit(solution)/shard_map/ppermute | solution.py:30
  1083.4 32.1 %collective-permute-done.48 = f32[640,1024]{1,0:T(8,128)} collective-permute-done((f32[640,1024]{1,0:T(8,128)}, f32[640,1024]{1,0:T(8,128)}, u32[]{:S(2)}, u32[]{:S(2)}) %collective-permute-start.48) | collective-permute-done | bytes 2621472 | tf_op jit(solution)/shard_map/ppermute | solution.py:30
  1133.7 10.3 collective-permute-done.43
  1145.8 26.2 %collective-permute-done.49 = f32[320,1024]{1,0:T(8,128)S(1)} collective-permute-done((f32[320,1024]{1,0:T(8,128)S(1)}, f32[320,1024]{1,0:T(8,128)S(1)}, u32[]{:S(2)}, u32[]{:S(2)}) %collective-permute-start.49) | collective-permute-done | bytes 1310752 | tf_op jit(solution)/shard_map/ppermute | solution.py:30
  1172.0 9.8 collective-permute-start.44
  1182.4 17.7 %collective-permute-done.23 = f32[128,2560]{1,0:T(8,128)S(1)} collective-permute-done((f32[128,2560]{1,0:T(8,128)}, f32[128,2560]{1,0:T(8,128)S(1)}, u32[]{:S(2)}, u32[]{:S(2)}) %collective-permute-start.23) | collective-permute-done | bytes 1310752 | tf_op jit(solution)/shard_map/ppermute | solution.py:30
  1200.1 9.8 collective-permute-start.50
  1210.4 17.8 %collective-permute-done.33 = f32[128,2560]{1,0:T(8,128)S(1)} collective-permute-done((f32[128,2560]{1,0:T(8,128)}, f32[128,2560]{1,0:T(8,128)S(1)}, u32[]{:S(2)}, u32[]{:S(2)}) %collective-permute-start.33) | collective-permute-done | bytes 1310752 | tf_op jit(solution)/shard_map/ppermute | solution.py:30
  1228.6 18.7 %collective-permute-start.45 = (f32[80,1024]{1,0:T(8,128)S(1)}, f32[80,1024]{1,0:T(8,128)S(1)}, u32[]{:S(2)}, u32[]{:S(2)}) collective-permute-start(f32[80,1024]{1,0:T(8,128)S(1)} %slice.638), channel_id=1, source_target_pairs={{0,8},{1,9},{2,10},{3,11},{4,12},{5,13},{6,14},{7,15},{8,0},{9,1},... | collective-permute-start | bytes 983048 | tf_op jit(solution)/shard_map/ppermute | solution.py:30
  1247.4 20.4 %collective-permute-start.51 = (f32[80,1024]{1,0:T(8,128)S(1)}, f32[80,1024]{1,0:T(8,128)S(1)}, u32[]{:S(2)}, u32[]{:S(2)}) collective-permute-start(f32[80,1024]{1,0:T(8,128)S(1)} %slice.640), channel_id=1, source_target_pairs={{0,8},{1,9},{2,10},{3,11},{4,12},{5,13},{6,14},{7,15},{8,0},{9,1},... | collective-permute-start | bytes 983048 | tf_op jit(solution)/shard_map/ppermute | solution.py:30
  1271.2 13.8 collective-permute-done.51
  1288.2 29.6 %collective-permute-done.28 = f32[64,5120]{1,0:T(8,128)S(1)} collective-permute-done((f32[64,5120]{1,0:T(8,128)S(1)}, f32[64,5120]{1,0:T(8,128)S(1)}, u32[]{:S(2)}, u32[]{:S(2)}) %collective-permute-start.28) | collective-permute-done | bytes 1310752 | tf_op jit(solution)/shard_map/ppermute | solution.py:30
  1318.0 6.2 collective-permute-start.29
  1324.1 21.8 %collective-permute-done.38 = f32[64,5120]{1,0:T(8,128)S(1)} collective-permute-done((f32[64,5120]{1,0:T(8,128)S(1)}, f32[64,5120]{1,0:T(8,128)S(1)}, u32[]{:S(2)}, u32[]{:S(2)}) %collective-permute-start.38) | collective-permute-done | bytes 1310752 | tf_op jit(solution)/shard_map/ppermute | solution.py:30
  1346.1 6.2 collective-permute-start.39
  1352.2 13.3 collective-permute-done.29
  1365.7 13.9 collective-permute-done.39
  (696 shorter events, 438.6 us)
Async XLA Ops:
  507.1 223.6 %collective-permute-start.10 = (f32[256,1664]{1,0:T(8,128)}, f32[256,1664]{1,0:T(8,128)}, u32[]{:S(2)}, u32[]{:S(2)}) collective-permute-start(f32[256,1664]{1,0:T(8,128)} %convolution_add_fusion.10), channel_id=1, source_target_pairs={{0,1},{1,0},{2,3},{3,2},{4,5},{5,4},{6,7},{7,6},{8,9},{9,8},{10,11... | collective-permute-start | bytes 5111816 | tf_op jit(solution)/shard_map/ppermute | solution.py:30
  511.7 196.1 %collective-permute-start.14 = (f32[256,1024]{1,0:T(8,128)}, f32[256,1024]{1,0:T(8,128)}, u32[]{:S(2)}, u32[]{:S(2)}) collective-permute-start(f32[256,1024]{1,0:T(8,128)} %fusion.263), channel_id=1, source_target_pairs={{0,1},{1,0},{2,3},{3,2},{4,5},{5,4},{6,7},{7,6},{8,9},{9,8},{10,11... | collective-permute-start | bytes 3145736 | tf_op jit(solution)/shard_map/ppermute | solution.py:30
  513.9 194.4 %collective-permute-start.15 = (f32[256,1024]{1,0:T(8,128)}, f32[256,1024]{1,0:T(8,128)}, u32[]{:S(2)}, u32[]{:S(2)}) collective-permute-start(f32[256,1024]{1,0:T(8,128)} %fusion.260), channel_id=1, source_target_pairs={{0,1},{1,0},{2,3},{3,2},{4,5},{5,4},{6,7},{7,6},{8,9},{9,8},{10,11... | collective-permute-start | bytes 3145736 | tf_op jit(solution)/shard_map/ppermute | solution.py:30
  560.8 155.7 %collective-permute-start.4 = (f32[256,1024]{1,0:T(8,128)}, f32[256,1024]{1,0:T(8,128)}, u32[]{:S(2)}, u32[]{:S(2)}) collective-permute-start(f32[256,1024]{1,0:T(8,128)} %fusion.273), channel_id=1, source_target_pairs={{0,1},{1,0},{2,3},{3,2},{4,5},{5,4},{6,7},{7,6},{8,9},{9,8},{10,11... | collective-permute-start | bytes 3145736 | tf_op jit(solution)/shard_map/ppermute | solution.py:30
  562.9 159.8 %collective-permute-start.5 = (f32[256,1024]{1,0:T(8,128)}, f32[256,1024]{1,0:T(8,128)}, u32[]{:S(2)}, u32[]{:S(2)}) collective-permute-start(f32[256,1024]{1,0:T(8,128)} %fusion.270), channel_id=1, source_target_pairs={{0,1},{1,0},{2,3},{3,2},{4,5},{5,4},{6,7},{7,6},{8,9},{9,8},{10,11... | collective-permute-start | bytes 3145736 | tf_op jit(solution)/shard_map/ppermute | solution.py:30
  707.9 30.2 %collective-permute-start.11 = (f32[256,1664]{1,0:T(8,128)}, f32[256,1664]{1,0:T(8,128)}, u32[]{:S(2)}, u32[]{:S(2)}) collective-permute-start(f32[256,1664]{1,0:T(8,128)} %convolution_add_fusion.8), channel_id=1, source_target_pairs={{0,1},{1,0},{2,3},{3,2},{4,5},{5,4},{6,7},{7,6},{8,9},{9,8},{10,11... | collective-permute-start | bytes 5111816 | tf_op jit(solution)/shard_map/ppermute | solution.py:30
  708.3 30.6 %collective-permute-start.1 = (f32[256,1664]{1,0:T(8,128)}, f32[256,1664]{1,0:T(8,128)}, u32[]{:S(2)}, u32[]{:S(2)}) collective-permute-start(f32[256,1664]{1,0:T(8,128)} %convolution_add_fusion.12), channel_id=1, source_target_pairs={{0,1},{1,0},{2,3},{3,2},{4,5},{5,4},{6,7},{7,6},{8,9},{9,8},{10,11... | collective-permute-start | bytes 5111816 | tf_op jit(solution)/shard_map/ppermute | solution.py:30
  716.5 62.8 %collective-permute-start.21 = (f32[256,2560]{1,0:T(8,128)}, f32[256,2560]{1,0:T(8,128)S(1)}, u32[]{:S(2)}, u32[]{:S(2)}) collective-permute-start(f32[256,2560]{1,0:T(8,128)} %fusion.254), channel_id=1, source_target_pairs={{0,1},{1,0},{2,3},{3,2},{4,5},{5,4},{6,7},{7,6},{8,9},{9,8},{10,11... | collective-permute-start | bytes 7864328 | tf_op jit(solution)/shard_map/ppermute | solution.py:30
  722.7 59.6 %collective-permute-start.25 = (f32[256,2560]{1,0:T(8,128)S(1)}, f32[256,2560]{1,0:T(8,128)S(1)}, u32[]{:S(2)}, u32[]{:S(2)}) collective-permute-start(f32[256,2560]{1,0:T(8,128)S(1)} %copy-done.58), channel_id=1, source_target_pairs={{0,1},{1,0},{2,3},{3,2},{4,5},{5,4},{6,7},{7,6},{8,9},{9,8},{10,11... | collective-permute-start | bytes 7864328 | tf_op jit(solution)/shard_map/ppermute | solution.py:30
  730.7 25.0 %collective-permute-start.16 = (f32[256,1024]{1,0:T(8,128)S(1)}, f32[256,1024]{1,0:T(8,128)S(1)}, u32[]{:S(2)}, u32[]{:S(2)}) collective-permute-start(f32[256,1024]{1,0:T(8,128)S(1)} %convolution_add_fusion.18), channel_id=1, source_target_pairs={{0,4},{1,5},{2,6},{3,7},{4,0},{5,1},{6,2},{7,3},{8,12},{9,13},{10,... | collective-permute-start | bytes 3145736 | tf_op jit(solution)/shard_map/ppermute | solution.py:30
  738.1 57.9 %collective-permute-start.31 = (f32[256,2560]{1,0:T(8,128)}, f32[256,2560]{1,0:T(8,128)}, u32[]{:S(2)}, u32[]{:S(2)}) collective-permute-start(f32[256,2560]{1,0:T(8,128)} %fusion.242), channel_id=1, source_target_pairs={{0,1},{1,0},{2,3},{3,2},{4,5},{5,4},{6,7},{7,6},{8,9},{9,8},{10,11... | collective-permute-start | bytes 7864328 | tf_op jit(solution)/shard_map/ppermute | solution.py:30
  738.9 39.3 %collective-permute-start.6 = (f32[256,1024]{1,0:T(8,128)S(1)}, f32[256,1024]{1,0:T(8,128)S(1)}, u32[]{:S(2)}, u32[]{:S(2)}) collective-permute-start(f32[256,1024]{1,0:T(8,128)S(1)} %convolution_add_fusion.20), channel_id=1, source_target_pairs={{0,4},{1,5},{2,6},{3,7},{4,0},{5,1},{6,2},{7,3},{8,12},{9,13},{10,... | collective-permute-start | bytes 3145736 | tf_op jit(solution)/shard_map/ppermute | solution.py:30
  755.7 46.7 %collective-permute-start.41 = (f32[640,1024]{1,0:T(8,128)}, f32[640,1024]{1,0:T(8,128)}, u32[]{:S(2)}, u32[]{:S(2)}) collective-permute-start(f32[640,1024]{1,0:T(8,128)} %get-tuple-element.91), channel_id=1, source_target_pairs={{0,1},{1,0},{2,3},{3,2},{4,5},{5,4},{6,7},{7,6},{8,9},{9,8},{10,11... | collective-permute-start | bytes 7864328 | tf_op jit(solution)/shard_map/ppermute | solution.py:30
  779.3 28.2 %collective-permute-start.47 = (f32[640,1024]{1,0:T(8,128)}, f32[640,1024]{1,0:T(8,128)S(1)}, u32[]{:S(2)}, u32[]{:S(2)}) collective-permute-start(f32[640,1024]{1,0:T(8,128)} %get-tuple-element.93), channel_id=1, source_target_pairs={{0,1},{1,0},{2,3},{3,2},{4,5},{5,4},{6,7},{7,6},{8,9},{9,8},{10,11... | collective-permute-start | bytes 7864328 | tf_op jit(solution)/shard_map/ppermute | solution.py:30
  782.3 34.5 %collective-permute-start.35 = (f32[256,2560]{1,0:T(8,128)}, f32[256,2560]{1,0:T(8,128)}, u32[]{:S(2)}, u32[]{:S(2)}) collective-permute-start(f32[256,2560]{1,0:T(8,128)} %fusion.236), channel_id=1, source_target_pairs={{0,1},{1,0},{2,3},{3,2},{4,5},{5,4},{6,7},{7,6},{8,9},{9,8},{10,11... | collective-permute-start | bytes 7864328 | tf_op jit(solution)/shard_map/ppermute | solution.py:30
  795.9 50.7 %collective-permute-start.40 = (f32[640,1024]{1,0:T(8,128)}, f32[640,1024]{1,0:T(8,128)}, u32[]{:S(2)}, u32[]{:S(2)}) collective-permute-start(f32[640,1024]{1,0:T(8,128)} %get-tuple-element.90), channel_id=1, source_target_pairs={{0,1},{1,0},{2,3},{3,2},{4,5},{5,4},{6,7},{7,6},{8,9},{9,8},{10,11... | collective-permute-start | bytes 7864328 | tf_op jit(solution)/shard_map/ppermute | solution.py:30
  796.0 38.7 %collective-permute-start.12 = (f32[256,1664]{1,0:T(8,128)}, f32[256,1664]{1,0:T(8,128)}, u32[]{:S(2)}, u32[]{:S(2)}) collective-permute-start(f32[256,1664]{1,0:T(8,128)} %fusion.105), channel_id=1, source_target_pairs={{0,4},{1,5},{2,6},{3,7},{4,0},{5,1},{6,2},{7,3},{8,12},{9,13},{10,... | collective-permute-start | bytes 5111816 | tf_op jit(solution)/shard_map/ppermute | solution.py:30
  807.4 63.8 %collective-permute-start.2 = (f32[256,1664]{1,0:T(8,128)}, f32[256,1664]{1,0:T(8,128)}, u32[]{:S(2)}, u32[]{:S(2)}) collective-permute-start(f32[256,1664]{1,0:T(8,128)} %fusion.103), channel_id=1, source_target_pairs={{0,4},{1,5},{2,6},{3,7},{4,0},{5,1},{6,2},{7,3},{8,12},{9,13},{10,... | collective-permute-start | bytes 5111816 | tf_op jit(solution)/shard_map/ppermute | solution.py:30
  815.4 64.8 %collective-permute-start.20 = (f32[256,2560]{1,0:T(8,128)}, f32[256,2560]{1,0:T(8,128)}, u32[]{:S(2)}, u32[]{:S(2)}) collective-permute-start(f32[256,2560]{1,0:T(8,128)} %fusion.257), channel_id=1, source_target_pairs={{0,1},{1,0},{2,3},{3,2},{4,5},{5,4},{6,7},{7,6},{8,9},{9,8},{10,11... | collective-permute-start | bytes 7864328 | tf_op jit(solution)/shard_map/ppermute | solution.py:30
  816.8 64.9 %collective-permute-start.24 = (f32[256,2560]{1,0:T(8,128)}, f32[256,2560]{1,0:T(8,128)}, u32[]{:S(2)}, u32[]{:S(2)}) collective-permute-start(f32[256,2560]{1,0:T(8,128)} %fusion.251), channel_id=1, source_target_pairs={{0,1},{1,0},{2,3},{3,2},{4,5},{5,4},{6,7},{7,6},{8,9},{9,8},{10,11... | collective-permute-start | bytes 7864328 | tf_op jit(solution)/shard_map/ppermute | solution.py:30
  846.4 29.6 %collective-permute-start.13 = (f32[128,1664]{1,0:T(8,128)}, f32[128,1664]{1,0:T(8,128)}, u32[]{:S(2)}, u32[]{:S(2)}) collective-permute-start(f32[128,1664]{1,0:T(8,128)} %slice.581), channel_id=1, source_target_pairs={{0,2},{1,3},{2,0},{3,1},{4,6},{5,7},{6,4},{7,5},{8,10},{9,11},{10,... | collective-permute-start | bytes 2555912 | tf_op jit(solution)/shard_map/ppermute | solution.py:30
  846.6 137.6 %collective-permute-start.30 = (f32[256,2560]{1,0:T(8,128)}, f32[256,2560]{1,0:T(8,128)}, u32[]{:S(2)}, u32[]{:S(2)}) collective-permute-start(f32[256,2560]{1,0:T(8,128)} %fusion.245), channel_id=1, source_target_pairs={{0,1},{1,0},{2,3},{3,2},{4,5},{5,4},{6,7},{7,6},{8,9},{9,8},{10,11... | collective-permute-start | bytes 7864328 | tf_op jit(solution)/shard_map/ppermute | solution.py:30
  871.2 127.7 %collective-permute-start.22 = (f32[256,2560]{1,0:T(8,128)}, f32[256,2560]{1,0:T(8,128)}, u32[]{:S(2)}, u32[]{:S(2)}) collective-permute-start(f32[256,2560]{1,0:T(8,128)} %convolution_add_fusion.6), channel_id=1, source_target_pairs={{0,2},{1,3},{2,0},{3,1},{4,6},{5,7},{6,4},{7,5},{8,10},{9,11},{10,... | collective-permute-start | bytes 7864328 | tf_op jit(solution)/shard_map/ppermute | solution.py:30
  877.1 69.8 %collective-permute-start.3 = (f32[128,1664]{1,0:T(8,128)S(1)}, f32[128,1664]{1,0:T(8,128)S(1)}, u32[]{:S(2)}, u32[]{:S(2)}) collective-permute-start(f32[128,1664]{1,0:T(8,128)S(1)} %slice.564), channel_id=1, source_target_pairs={{0,2},{1,3},{2,0},{3,1},{4,6},{5,7},{6,4},{7,5},{8,10},{9,11},{10,... | collective-permute-start | bytes 2555912 | tf_op jit(solution)/shard_map/ppermute | solution.py:30
  880.2 120.7 %collective-permute-start.26 = (f32[256,2560]{1,0:T(8,128)S(1)}, f32[256,2560]{1,0:T(8,128)S(1)}, u32[]{:S(2)}, u32[]{:S(2)}) collective-permute-start(f32[256,2560]{1,0:T(8,128)S(1)} %copy-done.59), channel_id=1, source_target_pairs={{0,4},{1,5},{2,6},{3,7},{4,0},{5,1},{6,2},{7,3},{8,12},{9,13},{10,... | collective-permute-start | bytes 7864328 | tf_op jit(solution)/shard_map/ppermute | solution.py:30
  881.7 124.2 %collective-permute-start.32 = (f32[256,2560]{1,0:T(8,128)}, f32[256,2560]{1,0:T(8,128)S(1)}, u32[]{:S(2)}, u32[]{:S(2)}) collective-permute-start(f32[256,2560]{1,0:T(8,128)} %convolution_add_fusion.2), channel_id=1, source_target_pairs={{0,2},{1,3},{2,0},{3,1},{4,6},{5,7},{6,4},{7,5},{8,10},{9,11},{10,... | collective-permute-start | bytes 7864328 | tf_op jit(solution)/shard_map/ppermute | solution.py:30
  946.8 37.3 %collective-permute-start.18 = (f32[64,2688]{1,0:T(8,128)S(1)}, f32[64,2688]{1,0:T(8,128)S(1)}, u32[]{:S(2)}, u32[]{:S(2)}) collective-permute-start(f32[64,2688]{1,0:T(8,128)S(1)} %pad_maximum_fusion.10), channel_id=1, source_target_pairs={{0,16},{1,17},{2,18},{3,19},{4,20},{5,21},{6,22},{7,23},{8,24},{9,... | collective-permute-start | bytes 2064392 | tf_op jit(solution)/shard_map/ppermute | solution.py:30
  984.3 99.1 %collective-permute-start.46 = (f32[640,1024]{1,0:T(8,128)}, f32[640,1024]{1,0:T(8,128)}, u32[]{:S(2)}, u32[]{:S(2)}) collective-permute-start(f32[640,1024]{1,0:T(8,128)} %get-tuple-element.92), channel_id=1, source_target_pairs={{0,1},{1,0},{2,3},{3,2},{4,5},{5,4},{6,7},{7,6},{8,9},{9,8},{10,11... | collective-permute-start | bytes 7864328 | tf_op jit(solution)/shard_map/ppermute | solution.py:30
  998.5 60.8 %collective-permute-start.42 = (f32[640,1024]{1,0:T(8,128)}, f32[640,1024]{1,0:T(8,128)}, u32[]{:S(2)}, u32[]{:S(2)}) collective-permute-start(f32[640,1024]{1,0:T(8,128)} %bitcast_add_fusion.3), channel_id=1, source_target_pairs={{0,2},{1,3},{2,0},{3,1},{4,6},{5,7},{6,4},{7,5},{8,10},{9,11},{10,... | collective-permute-start | bytes 7864328 | tf_op jit(solution)/shard_map/ppermute | solution.py:30
  998.9 116.5 %collective-permute-start.48 = (f32[640,1024]{1,0:T(8,128)}, f32[640,1024]{1,0:T(8,128)}, u32[]{:S(2)}, u32[]{:S(2)}) collective-permute-start(f32[640,1024]{1,0:T(8,128)} %bitcast_add_fusion.1), channel_id=1, source_target_pairs={{0,2},{1,3},{2,0},{3,1},{4,6},{5,7},{6,4},{7,5},{8,10},{9,11},{10,... | collective-permute-start | bytes 7864328 | tf_op jit(solution)/shard_map/ppermute | solution.py:30
  1000.9 119.6 %collective-permute-start.34 = (f32[256,2560]{1,0:T(8,128)}, f32[256,2560]{1,0:T(8,128)}, u32[]{:S(2)}, u32[]{:S(2)}) collective-permute-start(f32[256,2560]{1,0:T(8,128)} %fusion.239), channel_id=1, source_target_pairs={{0,1},{1,0},{2,3},{3,2},{4,5},{5,4},{6,7},{7,6},{8,9},{9,8},{10,11... | collective-permute-start | bytes 7864328 | tf_op jit(solution)/shard_map/ppermute | solution.py:30
  1006.0 114.6 %collective-permute-start.36 = (f32[256,2560]{1,0:T(8,128)}, f32[256,2560]{1,0:T(8,128)}, u32[]{:S(2)}, u32[]{:S(2)}) collective-permute-start(f32[256,2560]{1,0:T(8,128)} %convolution_add_fusion), channel_id=1, source_target_pairs={{0,4},{1,5},{2,6},{3,7},{4,0},{5,1},{6,2},{7,3},{8,12},{9,13},{10,... | collective-permute-start | bytes 7864328 | tf_op jit(solution)/shard_map/ppermute | solution.py:30
  1059.3 67.2 %collective-permute-start.19 = (f32[32,2688]{1,0:T(8,128)}, f32[32,2688]{1,0:T(8,128)S(1)}, u32[]{:S(2)}, u32[]{:S(2)}) collective-permute-start(f32[32,2688]{1,0:T(8,128)} %slice.591), channel_id=1, source_target_pairs={{0,8},{1,9},{2,10},{3,11},{4,12},{5,13},{6,14},{7,15},{8,0},{9,1},... | collective-permute-start | bytes 1032200 | tf_op jit(solution)/shard_map/ppermute | solution.py:30
  1083.4 43.3 %collective-permute-start.9 = (f32[32,2688]{1,0:T(8,128)S(1)}, f32[32,2688]{1,0:T(8,128)S(1)}, u32[]{:S(2)}, u32[]{:S(2)}) collective-permute-start(f32[32,2688]{1,0:T(8,128)S(1)} %slice.574), channel_id=1, source_target_pairs={{0,8},{1,9},{2,10},{3,11},{4,12},{5,13},{6,14},{7,15},{8,0},{9,1},... | collective-permute-start | bytes 1032200 | tf_op jit(solution)/shard_map/ppermute | solution.py:30
  1115.5 28.5 %collective-permute-start.43 = (f32[320,1024]{1,0:T(8,128)}, f32[320,1024]{1,0:T(8,128)}, u32[]{:S(2)}, u32[]{:S(2)}) collective-permute-start(f32[320,1024]{1,0:T(8,128)} %dynamic-slice_bitcast_fusion.5), channel_id=1, source_target_pairs={{0,4},{1,5},{2,6},{3,7},{4,0},{5,1},{6,2},{7,3},{8,12},{9,13},{10,... | collective-permute-start | bytes 3932168 | tf_op jit(solution)/shard_map/ppermute | solution.py:30
  1120.5 51.5 %collective-permute-start.49 = (f32[320,1024]{1,0:T(8,128)S(1)}, f32[320,1024]{1,0:T(8,128)S(1)}, u32[]{:S(2)}, u32[]{:S(2)}) collective-permute-start(f32[320,1024]{1,0:T(8,128)S(1)} %dynamic-slice_bitcast_fusion.4), channel_id=1, source_target_pairs={{0,4},{1,5},{2,6},{3,7},{4,0},{5,1},{6,2},{7,3},{8,12},{9,13},{10,... | collective-permute-start | bytes 3932168 | tf_op jit(solution)/shard_map/ppermute | solution.py:30
  1120.6 79.5 %collective-permute-start.23 = (f32[128,2560]{1,0:T(8,128)}, f32[128,2560]{1,0:T(8,128)S(1)}, u32[]{:S(2)}, u32[]{:S(2)}) collective-permute-start(f32[128,2560]{1,0:T(8,128)} %slice.606), channel_id=1, source_target_pairs={{0,4},{1,5},{2,6},{3,7},{4,0},{5,1},{6,2},{7,3},{8,12},{9,13},{10,... | collective-permute-start | bytes 3932168 | tf_op jit(solution)/shard_map/ppermute | solution.py:30
  1126.6 83.5 %collective-permute-start.27 = (f32[128,2560]{1,0:T(8,128)S(1)}, f32[128,2560]{1,0:T(8,128)S(1)}, u32[]{:S(2)}, u32[]{:S(2)}) collective-permute-start(f32[128,2560]{1,0:T(8,128)S(1)} %copy-done.91), channel_id=1, source_target_pairs={{0,2},{1,3},{2,0},{3,1},{4,6},{5,7},{6,4},{7,5},{8,10},{9,11},{10,... | collective-permute-start | bytes 3932168 | tf_op jit(solution)/shard_map/ppermute | solution.py:30
  1126.7 101.5 %collective-permute-start.33 = (f32[128,2560]{1,0:T(8,128)}, f32[128,2560]{1,0:T(8,128)S(1)}, u32[]{:S(2)}, u32[]{:S(2)}) collective-permute-start(f32[128,2560]{1,0:T(8,128)} %slice.623), channel_id=1, source_target_pairs={{0,4},{1,5},{2,6},{3,7},{4,0},{5,1},{6,2},{7,3},{8,12},{9,13},{10,... | collective-permute-start | bytes 3932168 | tf_op jit(solution)/shard_map/ppermute | solution.py:30
  1144.0 84.3 %collective-permute-start.37 = (f32[128,2560]{1,0:T(8,128)S(1)}, f32[128,2560]{1,0:T(8,128)S(1)}, u32[]{:S(2)}, u32[]{:S(2)}) collective-permute-start(f32[128,2560]{1,0:T(8,128)S(1)} %slice.629), channel_id=1, source_target_pairs={{0,2},{1,3},{2,0},{3,1},{4,6},{5,7},{6,4},{7,5},{8,10},{9,11},{10,... | collective-permute-start | bytes 3932168 | tf_op jit(solution)/shard_map/ppermute | solution.py:30
  1172.0 56.5 %collective-permute-start.44 = (f32[160,1024]{1,0:T(8,128)S(1)}, f32[160,1024]{1,0:T(8,128)S(1)}, u32[]{:S(2)}, u32[]{:S(2)}) collective-permute-start(f32[160,1024]{1,0:T(8,128)S(1)} %pad_maximum_fusion.16), channel_id=1, source_target_pairs={{0,16},{1,17},{2,18},{3,19},{4,20},{5,21},{6,22},{7,23},{8,24},{9,... | collective-permute-start | bytes 1966088 | tf_op jit(solution)/shard_map/ppermute | solution.py:30
  1200.1 47.3 %collective-permute-start.50 = (f32[160,1024]{1,0:T(8,128)S(1)}, f32[160,1024]{1,0:T(8,128)S(1)}, u32[]{:S(2)}, u32[]{:S(2)}) collective-permute-start(f32[160,1024]{1,0:T(8,128)S(1)} %pad_maximum_fusion.17), channel_id=1, source_target_pairs={{0,16},{1,17},{2,18},{3,19},{4,20},{5,21},{6,22},{7,23},{8,24},{9,... | collective-permute-start | bytes 1966088 | tf_op jit(solution)/shard_map/ppermute | solution.py:30
  1210.3 107.5 %collective-permute-start.28 = (f32[64,5120]{1,0:T(8,128)S(1)}, f32[64,5120]{1,0:T(8,128)S(1)}, u32[]{:S(2)}, u32[]{:S(2)}) collective-permute-start(f32[64,5120]{1,0:T(8,128)S(1)} %pad_maximum_fusion.5), channel_id=1, source_target_pairs={{0,16},{1,17},{2,18},{3,19},{4,20},{5,21},{6,22},{7,23},{8,24},{9,... | collective-permute-start | bytes 3932168 | tf_op jit(solution)/shard_map/ppermute | solution.py:30
  1228.6 42.5 %collective-permute-start.45 = (f32[80,1024]{1,0:T(8,128)S(1)}, f32[80,1024]{1,0:T(8,128)S(1)}, u32[]{:S(2)}, u32[]{:S(2)}) collective-permute-start(f32[80,1024]{1,0:T(8,128)S(1)} %slice.638), channel_id=1, source_target_pairs={{0,8},{1,9},{2,10},{3,11},{4,12},{5,13},{6,14},{7,15},{8,0},{9,1},... | collective-permute-start | bytes 983048 | tf_op jit(solution)/shard_map/ppermute | solution.py:30
  1247.4 37.6 %collective-permute-start.51 = (f32[80,1024]{1,0:T(8,128)S(1)}, f32[80,1024]{1,0:T(8,128)S(1)}, u32[]{:S(2)}, u32[]{:S(2)}) collective-permute-start(f32[80,1024]{1,0:T(8,128)S(1)} %slice.640), channel_id=1, source_target_pairs={{0,8},{1,9},{2,10},{3,11},{4,12},{5,13},{6,14},{7,15},{8,0},{9,1},... | collective-permute-start | bytes 983048 | tf_op jit(solution)/shard_map/ppermute | solution.py:30
  1267.9 78.0 %collective-permute-start.38 = (f32[64,5120]{1,0:T(8,128)S(1)}, f32[64,5120]{1,0:T(8,128)S(1)}, u32[]{:S(2)}, u32[]{:S(2)}) collective-permute-start(f32[64,5120]{1,0:T(8,128)S(1)} %pad_maximum_fusion.4), channel_id=1, source_target_pairs={{0,16},{1,17},{2,18},{3,19},{4,20},{5,21},{6,22},{7,23},{8,24},{9,... | collective-permute-start | bytes 3932168 | tf_op jit(solution)/shard_map/ppermute | solution.py:30
  1318.0 47.6 %collective-permute-start.29 = (f32[32,5120]{1,0:T(8,128)S(1)}, f32[32,5120]{1,0:T(8,128)S(1)}, u32[]{:S(2)}, u32[]{:S(2)}) collective-permute-start(f32[32,5120]{1,0:T(8,128)S(1)} %slice.616), channel_id=1, source_target_pairs={{0,8},{1,9},{2,10},{3,11},{4,12},{5,13},{6,14},{7,15},{8,0},{9,1},... | collective-permute-start | bytes 1966088 | tf_op jit(solution)/shard_map/ppermute | solution.py:30
  1346.1 33.5 %collective-permute-start.39 = (f32[32,5120]{1,0:T(8,128)S(1)}, f32[32,5120]{1,0:T(8,128)S(1)}, u32[]{:S(2)}, u32[]{:S(2)}) collective-permute-start(f32[32,5120]{1,0:T(8,128)S(1)} %slice.633), channel_id=1, source_target_pairs={{0,8},{1,9},{2,10},{3,11},{4,12},{5,13},{6,14},{7,15},{8,0},{9,1},... | collective-permute-start | bytes 1966088 | tf_op jit(solution)/shard_map/ppermute | solution.py:30
  (180 other events, 2275.6 us)

commit v2 on v1

--- a/solution.py
+++ b/solution.py
@@ -133,10 +133,10 @@
 
 
 def scatter_z(part):
-    half = part.shape[0] // 2
-    part = part[:half] + send(part[half:], 16)
-    half = half // 2
-    return part[:half] + send(part[half:], 8)
+    rows = part.shape[0] // 4
+    blocks = [part[step * rows:(step + 1) * rows] for step in range(4)]
+    got = send(jnp.concatenate([blocks[1], blocks[3]]), 8)
+    return blocks[0] + got[:rows] + send(blocks[2] + got[rows:], 16)
 
 
 def layer_backward(weights, rope_cos, rope_sin, saved, grad_out, batch, seq_len, place, to_rel, nat_to_rel):
@@ -194,18 +194,27 @@
     core_peer = me + 1 - 2 * core
     x_peer = me + 2 - 4 * x_at
     y_peer = me + 4 - 8 * y_at
-    z_peers = [(z_at + step) % 4 * 8 + me % 8 for step in (1, 2, 3)]
+    z_near = me + 8 - 16 * (z_at % 2)
+    z_far = me + 16 - 32 * (z_at // 2)
+    far_at = z_at + 2 - 4 * (z_at // 2)
     barrier = pltpu.get_barrier_semaphore()
-    for peer in (core_peer, x_peer, y_peer, *z_peers):
+    for peer in (core_peer, x_peer, y_peer, z_near, z_far):
         pl.semaphore_signal(barrier, inc=1, device_id=(peer,), device_id_type=pl.DeviceIdType.MESH)
-    pl.semaphore_wait(barrier, 6)
+    pl.semaphore_wait(barrier, 5)
 
     def copy(index, stage, source, target, peer):
         return pltpu.make_async_remote_copy(src_ref=source, dst_ref=target, send_sem=send_sem.at[index, stage], recv_sem=recv_sem.at[index, stage],
                                             device_id=(peer,), device_id_type=pl.DeviceIdType.MESH)
 
-    def z_copies(index):
-        return [copy(index, step, shards[index], wholes[index].at[core, x_at, y_at, z_at], z_peers[step]) for step in range(3)]
+    def to_near(index):
+        return copy(index, 0, shards[index], wholes[index].at[core, x_at, y_at, z_at], z_near)
+
+    def to_far(index):
+        return copy(index, 1, shards[index], wholes[index].at[core, x_at, y_at, z_at], z_far)
+
+    def onward(index):
+        part = wholes[index].at[core, x_at, y_at, far_at]
+        return copy(index, 2, part, part, z_near)
 
     def second(index):
         part = wholes[index].at[core, x_at, y_at]
@@ -225,27 +234,30 @@
     def own(index):
         return pltpu.make_async_copy(shards[index], wholes[index].at[core, x_at, y_at, z_at], own_sem.at[index])
 
-    for index in range(count):
-        own(index).start()
-        for one in z_copies(index):
-            one.start()
-    for index in range(count):
-        own(index).wait()
-        for one in z_copies(index):
-            one.wait()
-        second(index).start()
-        if index >= 2:
-            second(index - 2).wait()
-            third(index - 2).start()
-        if index >= 5:
-            third(index - 5).wait()
-            last(index - 5).start()
-    for index in (count - 2, count - 1):
-        second(index).wait()
-        third(index).start()
-    for index in range(count - 5, count):
-        third(index).wait()
-        last(index).start()
+    def begin(index):
+        if index < count:
+            own(index).start()
+            to_far(index).start()
+            to_near(index).start()
+
+    for index in range(3):
+        begin(index)
+    for turn in range(count + 6):
+        begin(turn + 3)
+        if turn < count:
+            to_far(turn).wait()
+            onward(turn).start()
+        if 0 <= turn - 1 < count:
+            own(turn - 1).wait()
+            to_near(turn - 1).wait()
+            onward(turn - 1).wait()
+            second(turn - 1).start()
+        if 0 <= turn - 3 < count:
+            second(turn - 3).wait()
+            third(turn - 3).start()
+        if 0 <= turn - 6 < count:
+            third(turn - 6).wait()
+            last(turn - 6).start()
     for index in range(count):
         last(index).wait()
 

time: 1400 us -> 1300 us (0.929)
  starting transfers between devices: 135 us -> 33.9 us
    ppermute x52, starting transfers between devices: 135 us -> 33.9 us  [send(): return lax.ppermute(values, 'fsdp', flip(bits))]
    unnamed x374 -> x386, local copies, waits for them, and re-layouts: 47 us -> 49.6 us
  transfers between devices with their start and end apart: 52 -> 52, of which waited for: 20 -> 23; matrix products, arithmetic and copies ran while one was open for 23% -> 29% of each run, Pallas kernels for 0% -> 0%
where the time goes in v2:
time: 1300 us
  matrix products  440 us (34%)
  waiting for transfers between devices  404 us (31%)
  Pallas kernels  231 us (18%)
  local copies, waits for them, and re-layouts  118 us (9%)
  other arithmetic  64.9 us (5%)
  starting transfers between devices  33.9 us (3%)
    ppermute x52, waiting for transfers between devices, send(): return lax.ppermute(values, 'fsdp', flip(bits))  404 us
    dot_general x69, matrix products, dot(): lax.dot_general(left, right, ((dims[:1], dims[1:]), ((), ())), preferred_...  359 us
    pallas_call x1, Pallas kernels, gather_all(): pl.pallas_call(gather_kernel, out_shape=[jax.ShapeDtypeStruct((2, 2, 2, 4...  231 us
    unnamed x386, local copies, waits for them, and re-layouts  49.6 us
    ppermute x52, starting transfers between devices, send(): return lax.ppermute(values, 'fsdp', flip(bits))  33.9 us
  transfers between devices with their start and end apart: 52, of which 23 were waited for; matrix products, arithmetic and copies ran while one was open for 29% of the time, Pallas kernels for 0%

profile of v2, /device:TPU:1, one launch (start us, length us, event | category | flops | bytes accessed | tf_op | source)
XLA Modules:
  0.0 1296.1 jit_solution(4732344026275479728)
XLA Ops:
  16.5 231.3 %shard_map.212 = (bf16[2,2,2,4,32,1664]{5,4,3,2,1,0:T(8,128)(2,1)S(1)}, bf16[2,2,2,4,32,1024]{5,4,3,2,1,0:T(8,128)(2,1)S(1)}, bf16[2,2,2,4,32,2560]{5,4,3,2,1,0:...) custom-call(bf16[32,1664]{1,0:T(8,128)(2,1)S(1)} %get-tuple-element., ...), custom_call_target="tpu_custom_call" | custom-call | tf_op jit(solution)/shard_map/pallas_call | solution.py:267
  277.9 5.5 copy.245
  307.3 11.4 fusion.395
  318.7 13.3 %multiply_convert_fusion.5 = (bf16[1024,2560]{1,0:T(8,128)(2,1)}, f32[1024,2560]{1,0:T(8,128)}) fusion(f32[1024,2560]{1,0:T(8,128)} %fusion.395, bf16[1024,2560]{1,0:T(8,128)(2,1)S(1)} %bitcast.528, bf16[1024,1024]{0,1:T(8,128)(2,1)S(1)} %copy-done.73, f32[1024]{0:T(1024)S(1)} %bitcast.661, f32[1024]{0:T(1024)S(1)} %add_rsqrt_fusion.2), kind=kOutput, calls=%fused_computation.18 | convolution fusion | flops 5388632064 | bytes 33562624 | tf_op jit(solution)/shard_map/dot_general | solution.py:47
  332.0 10.0 fusion.39
  344.5 5.8 fusion.232
  355.1 5.4 copy.257
  386.1 11.3 fusion.387
  397.5 8.8 fusion.389
  410.0 20.1 %multiply_convert_fusion.2 = (bf16[1024,2560]{1,0:T(8,128)(2,1)}, bf16[1024,2560]{1,0:T(8,128)(2,1)}, bf16[1024,2560]{1,0:T(8,128)(2,1)}) fusion(f32[1024,2560]{1,0:T(8,128)} %fusion.389, f32[1024,2560]{1,0:T(8,128)} %fusion.387, bf16[1024,1024]{1,0:T(8,128)(2,1)} %fusion.148, bf16[2560,1024]{1,0:T(8,128)(2,1)} %bitcast.524), kind=kOutput, calls=%fused_computation.14 | convolution fusion | flops 5410652160 | bytes 44040192 | tf_op jit(solution)/shard_map/dot_general | solution.py:47
  430.2 9.3 fusion.406
  439.5 9.7 fusion.46
  465.2 12.3 fusion.97
  477.6 12.3 fusion.191
  523.6 18.4 %multiply_convert_fusion = (bf16[1024,2560]{1,0:T(8,128)(2,1)}, bf16[1024,2560]{1,0:T(8,128)(2,1)}) fusion(f32[1024,2560]{1,0:T(8,128)} %fusion.395, f32[1024,2560]{1,0:T(8,128)} %get-tuple-element.157, bf16[1024,1024]{0,1:T(8,128)(2,1)} %fusion.37, bf16[2560,1024]{1,0:T(8,128)(2,1)} %bitcast.534), kind=kOutput, calls=%fused_computation.12 | convolution fusion | flops 5402787840 | bytes 38797312 | tf_op jit(solution)/shard_map/dot_general | solution.py:47
  542.0 9.7 fusion.407
  551.7 6.1 fusion.29
  572.1 12.5 fusion.95
  584.6 12.4 fusion.192
  613.3 6.5 fusion.59
  629.3 8.8 fusion.408
  669.4 8.6 fusion.409
  678.1 13.9 %convert_bitcast_fusion.3 = bf16[120,8,8,128]{3,2,1,0:T(8,128)(2,1)} fusion(s32[960]{0:T(1024)S(1)} %copy-done.130, bf16[1024,1024]{0,1:T(8,128)(2,1)} %get-tuple-element.163, bf16[1024,2560]{1,0:T(8,128)(2,1)} %get-tuple-element.89, bf16[2560,1024]{1,0:T(8,128)(2,1)} %bitcast.525), kind=kOutput, calls=%fused_computation.232 | convolution fusion | flops 7387086848 | bytes 14552832 | tf_op jit(solution)/shard_map/dot_general | solution.py:47
  692.0 10.1 convert_bitcast_fusion
  702.1 6.3 fusion.247
  714.5 5.9 dynamic-slice_bitcast_fusion.3
  720.6 5.9 fusion.244
  748.9 7.1 collective-permute-done.16
  757.4 7.3 fusion.103
  764.8 13.7 %collective-permute-done.6 = f32[256,1024]{1,0:T(8,128)S(1)} collective-permute-done((f32[256,1024]{1,0:T(8,128)S(1)}, f32[256,1024]{1,0:T(8,128)S(1)}, u32[]{:S(2)}, u32[]{:S(2)}) %collective-permute-start.6) | collective-permute-done | bytes 1048608 | tf_op jit(solution)/shard_map/ppermute | solution.py:30
  807.7 7.3 collective-permute-done.17
  826.7 8.7 collective-permute-done.12
  836.0 5.2 fusion.106
  848.3 23.5 %collective-permute-done.2 = f32[256,1664]{1,0:T(8,128)} collective-permute-done((f32[256,1664]{1,0:T(8,128)}, f32[256,1664]{1,0:T(8,128)}, u32[]{:S(2)}, u32[]{:S(2)}) %collective-permute-start.2) | collective-permute-done | bytes 1703968 | tf_op jit(solution)/shard_map/ppermute | solution.py:30
  883.3 15.8 %collective-permute-done.3 = f32[128,1664]{1,0:T(8,128)S(1)} collective-permute-done((f32[128,1664]{1,0:T(8,128)S(1)}, f32[128,1664]{1,0:T(8,128)S(1)}, u32[]{:S(2)}, u32[]{:S(2)}) %collective-permute-start.3) | collective-permute-done | bytes 852000 | tf_op jit(solution)/shard_map/ppermute | solution.py:30
  900.9 15.3 %collective-permute-done.18 = f32[64,2688]{1,0:T(8,128)S(1)} collective-permute-done((f32[64,2688]{1,0:T(8,128)S(1)}, f32[64,2688]{1,0:T(8,128)S(1)}, u32[]{:S(2)}, u32[]{:S(2)}) %collective-permute-start.18) | collective-permute-done | bytes 688160 | tf_op jit(solution)/shard_map/ppermute | solution.py:30
  919.7 11.0 collective-permute-done.8
  931.8 8.2 collective-permute-done.26
  941.3 13.9 %collective-permute-done.22 = f32[256,2560]{1,0:T(8,128)S(1)} collective-permute-done((f32[256,2560]{1,0:T(8,128)S(1)}, f32[256,2560]{1,0:T(8,128)S(1)}, u32[]{:S(2)}, u32[]{:S(2)}) %collective-permute-start.22) | collective-permute-done | bytes 2621472 | tf_op jit(solution)/shard_map/ppermute | solution.py:30
  956.6 39.7 %collective-permute-done.36 = f32[256,2560]{1,0:T(8,128)S(1)} collective-permute-done((f32[256,2560]{1,0:T(8,128)}, f32[256,2560]{1,0:T(8,128)S(1)}, u32[]{:S(2)}, u32[]{:S(2)}) %collective-permute-start.36) | collective-permute-done | bytes 2621472 | tf_op jit(solution)/shard_map/ppermute | solution.py:30
  1019.3 48.4 %collective-permute-done.48 = f32[640,1024]{1,0:T(8,128)} collective-permute-done((f32[640,1024]{1,0:T(8,128)}, f32[640,1024]{1,0:T(8,128)}, u32[]{:S(2)}, u32[]{:S(2)}) %collective-permute-start.48) | collective-permute-done | bytes 2621472 | tf_op jit(solution)/shard_map/ppermute | solution.py:30
  1073.6 50.3 %collective-permute-done.32 = f32[256,2560]{1,0:T(8,128)} collective-permute-done((f32[256,2560]{1,0:T(8,128)}, f32[256,2560]{1,0:T(8,128)}, u32[]{:S(2)}, u32[]{:S(2)}) %collective-permute-start.32) | collective-permute-done | bytes 2621472 | tf_op jit(solution)/shard_map/ppermute | solution.py:30
  1138.6 14.7 %collective-permute-done.27 = f32[128,2560]{1,0:T(8,128)S(1)} collective-permute-done((f32[128,2560]{1,0:T(8,128)S(1)}, f32[128,2560]{1,0:T(8,128)S(1)}, u32[]{:S(2)}, u32[]{:S(2)}) %collective-permute-start.27) | collective-permute-done | bytes 1310752 | tf_op jit(solution)/shard_map/ppermute | solution.py:30
  1158.6 22.9 %collective-permute-done.37 = f32[128,2560]{1,0:T(8,128)S(1)} collective-permute-done((f32[128,2560]{1,0:T(8,128)S(1)}, f32[128,2560]{1,0:T(8,128)S(1)}, u32[]{:S(2)}, u32[]{:S(2)}) %collective-permute-start.37) | collective-permute-done | bytes 1310752 | tf_op jit(solution)/shard_map/ppermute | solution.py:30
  1189.2 10.6 collective-permute-done.45
  1199.9 16.1 %collective-permute-done.51 = f32[80,1024]{1,0:T(8,128)S(1)} collective-permute-done((f32[80,1024]{1,0:T(8,128)S(1)}, f32[80,1024]{1,0:T(8,128)S(1)}, u32[]{:S(2)}, u32[]{:S(2)}) %collective-permute-start.51) | collective-permute-done | bytes 327712 | tf_op jit(solution)/shard_map/ppermute | solution.py:30
  1219.3 31.6 %collective-permute-done.38 = f32[64,5120]{1,0:T(8,128)S(1)} collective-permute-done((f32[64,5120]{1,0:T(8,128)S(1)}, f32[64,5120]{1,0:T(8,128)S(1)}, u32[]{:S(2)}, u32[]{:S(2)}) %collective-permute-start.38) | collective-permute-done | bytes 1310752 | tf_op jit(solution)/shard_map/ppermute | solution.py:30
  1251.2 30.4 %collective-permute-done.39 = f32[32,5120]{1,0:T(8,128)S(1)} collective-permute-done((f32[32,5120]{1,0:T(8,128)S(1)}, f32[32,5120]{1,0:T(8,128)S(1)}, u32[]{:S(2)}, u32[]{:S(2)}) %collective-permute-start.39) | collective-permute-done | bytes 655392 | tf_op jit(solution)/shard_map/ppermute | solution.py:30
  (706 shorter events, 398.8 us)
Async XLA Ops:
  455.8 258.3 %collective-permute-start.14 = (f32[256,1024]{1,0:T(8,128)}, f32[256,1024]{1,0:T(8,128)}, u32[]{:S(2)}, u32[]{:S(2)}) collective-permute-start(f32[256,1024]{1,0:T(8,128)} %fusion.265), channel_id=1, source_target_pairs={{0,1},{1,0},{2,3},{3,2},{4,5},{5,4},{6,7},{7,6},{8,9},{9,8},{10,11... | collective-permute-start | bytes 3145736 | tf_op jit(solution)/shard_map/ppermute | solution.py:30
  457.7 262.8 %collective-permute-start.15 = (f32[256,1024]{1,0:T(8,128)}, f32[256,1024]{1,0:T(8,128)}, u32[]{:S(2)}, u32[]{:S(2)}) collective-permute-start(f32[256,1024]{1,0:T(8,128)} %fusion.262), channel_id=1, source_target_pairs={{0,1},{1,0},{2,3},{3,2},{4,5},{5,4},{6,7},{7,6},{8,9},{9,8},{10,11... | collective-permute-start | bytes 3145736 | tf_op jit(solution)/shard_map/ppermute | solution.py:30
  515.8 226.6 %collective-permute-start.11 = (f32[256,1664]{1,0:T(8,128)}, f32[256,1664]{1,0:T(8,128)}, u32[]{:S(2)}, u32[]{:S(2)}) collective-permute-start(f32[256,1664]{1,0:T(8,128)} %convolution_add_fusion.8), channel_id=1, source_target_pairs={{0,1},{1,0},{2,3},{3,2},{4,5},{5,4},{6,7},{7,6},{8,9},{9,8},{10,11... | collective-permute-start | bytes 5111816 | tf_op jit(solution)/shard_map/ppermute | solution.py:30
  563.2 166.4 %collective-permute-start.4 = (f32[256,1024]{1,0:T(8,128)}, f32[256,1024]{1,0:T(8,128)}, u32[]{:S(2)}, u32[]{:S(2)}) collective-permute-start(f32[256,1024]{1,0:T(8,128)} %fusion.275), channel_id=1, source_target_pairs={{0,1},{1,0},{2,3},{3,2},{4,5},{5,4},{6,7},{7,6},{8,9},{9,8},{10,11... | collective-permute-start | bytes 3145736 | tf_op jit(solution)/shard_map/ppermute | solution.py:30
  625.2 117.5 %collective-permute-start.1 = (f32[256,1664]{1,0:T(8,128)}, f32[256,1664]{1,0:T(8,128)}, u32[]{:S(2)}, u32[]{:S(2)}) collective-permute-start(f32[256,1664]{1,0:T(8,128)} %convolution_add_fusion.12), channel_id=1, source_target_pairs={{0,1},{1,0},{2,3},{3,2},{4,5},{5,4},{6,7},{7,6},{8,9},{9,8},{10,11... | collective-permute-start | bytes 5111816 | tf_op jit(solution)/shard_map/ppermute | solution.py:30
  714.0 16.1 %collective-permute-start.5 = (f32[256,1024]{1,0:T(8,128)S(1)}, f32[256,1024]{1,0:T(8,128)S(1)}, u32[]{:S(2)}, u32[]{:S(2)}) collective-permute-start(f32[256,1024]{1,0:T(8,128)S(1)} %fusion.272), channel_id=1, source_target_pairs={{0,1},{1,0},{2,3},{3,2},{4,5},{5,4},{6,7},{7,6},{8,9},{9,8},{10,11... | collective-permute-start | bytes 3145736 | tf_op jit(solution)/shard_map/ppermute | solution.py:30
  720.5 61.2 %collective-permute-start.41 = (f32[640,1024]{1,0:T(8,128)}, f32[640,1024]{1,0:T(8,128)}, u32[]{:S(2)}, u32[]{:S(2)}) collective-permute-start(f32[640,1024]{1,0:T(8,128)} %get-tuple-element.91), channel_id=1, source_target_pairs={{0,1},{1,0},{2,3},{3,2},{4,5},{5,4},{6,7},{7,6},{8,9},{9,8},{10,11... | collective-permute-start | bytes 7864328 | tf_op jit(solution)/shard_map/ppermute | solution.py:30
  729.6 59.6 %collective-permute-start.25 = (f32[256,2560]{1,0:T(8,128)}, f32[256,2560]{1,0:T(8,128)}, u32[]{:S(2)}, u32[]{:S(2)}) collective-permute-start(f32[256,2560]{1,0:T(8,128)} %fusion.250), channel_id=1, source_target_pairs={{0,1},{1,0},{2,3},{3,2},{4,5},{5,4},{6,7},{7,6},{8,9},{9,8},{10,11... | collective-permute-start | bytes 7864328 | tf_op jit(solution)/shard_map/ppermute | solution.py:30
  731.1 24.9 %collective-permute-start.16 = (f32[256,1024]{1,0:T(8,128)}, f32[256,1024]{1,0:T(8,128)S(1)}, u32[]{:S(2)}, u32[]{:S(2)}) collective-permute-start(f32[256,1024]{1,0:T(8,128)} %convolution_add_fusion.18), channel_id=1, source_target_pairs={{0,4},{1,5},{2,6},{3,7},{4,0},{5,1},{6,2},{7,3},{8,12},{9,13},{10,... | collective-permute-start | bytes 3145736 | tf_op jit(solution)/shard_map/ppermute | solution.py:30
  742.3 52.5 %collective-permute-start.21 = (f32[256,2560]{1,0:T(8,128)S(1)}, f32[256,2560]{1,0:T(8,128)S(1)}, u32[]{:S(2)}, u32[]{:S(2)}) collective-permute-start(f32[256,2560]{1,0:T(8,128)S(1)} %copy-done.64), channel_id=1, source_target_pairs={{0,1},{1,0},{2,3},{3,2},{4,5},{5,4},{6,7},{7,6},{8,9},{9,8},{10,11... | collective-permute-start | bytes 7864328 | tf_op jit(solution)/shard_map/ppermute | solution.py:30
  742.7 35.7 %collective-permute-start.6 = (f32[256,1024]{1,0:T(8,128)S(1)}, f32[256,1024]{1,0:T(8,128)S(1)}, u32[]{:S(2)}, u32[]{:S(2)}) collective-permute-start(f32[256,1024]{1,0:T(8,128)S(1)} %convolution_add_fusion.20), channel_id=1, source_target_pairs={{0,4},{1,5},{2,6},{3,7},{4,0},{5,1},{6,2},{7,3},{8,12},{9,13},{10,... | collective-permute-start | bytes 3145736 | tf_op jit(solution)/shard_map/ppermute | solution.py:30
  756.0 45.7 %collective-permute-start.35 = (f32[256,2560]{1,0:T(8,128)S(1)}, f32[256,2560]{1,0:T(8,128)}, u32[]{:S(2)}, u32[]{:S(2)}) collective-permute-start(f32[256,2560]{1,0:T(8,128)S(1)} %copy-done.63), channel_id=1, source_target_pairs={{0,1},{1,0},{2,3},{3,2},{4,5},{5,4},{6,7},{7,6},{8,9},{9,8},{10,11... | collective-permute-start | bytes 7864328 | tf_op jit(solution)/shard_map/ppermute | solution.py:30
  778.4 37.6 %collective-permute-start.47 = (f32[640,1024]{1,0:T(8,128)}, f32[640,1024]{1,0:T(8,128)S(1)}, u32[]{:S(2)}, u32[]{:S(2)}) collective-permute-start(f32[640,1024]{1,0:T(8,128)} %get-tuple-element.93), channel_id=1, source_target_pairs={{0,1},{1,0},{2,3},{3,2},{4,5},{5,4},{6,7},{7,6},{8,9},{9,8},{10,11... | collective-permute-start | bytes 7864328 | tf_op jit(solution)/shard_map/ppermute | solution.py:30
  781.7 39.3 %collective-permute-start.31 = (f32[256,2560]{1,0:T(8,128)}, f32[256,2560]{1,0:T(8,128)}, u32[]{:S(2)}, u32[]{:S(2)}) collective-permute-start(f32[256,2560]{1,0:T(8,128)} %fusion.244), channel_id=1, source_target_pairs={{0,1},{1,0},{2,3},{3,2},{4,5},{5,4},{6,7},{7,6},{8,9},{9,8},{10,11... | collective-permute-start | bytes 7864328 | tf_op jit(solution)/shard_map/ppermute | solution.py:30
  789.3 37.2 %collective-permute-start.10 = (f32[256,1664]{1,0:T(8,128)S(1)}, f32[256,1664]{1,0:T(8,128)}, u32[]{:S(2)}, u32[]{:S(2)}) collective-permute-start(f32[256,1664]{1,0:T(8,128)S(1)} %copy-done.135), channel_id=1, source_target_pairs={{0,1},{1,0},{2,3},{3,2},{4,5},{5,4},{6,7},{7,6},{8,9},{9,8},{10,11... | collective-permute-start | bytes 5111816 | tf_op jit(solution)/shard_map/ppermute | solution.py:30
  796.3 39.1 %collective-permute-start.12 = (f32[256,1664]{1,0:T(8,128)}, f32[256,1664]{1,0:T(8,128)}, u32[]{:S(2)}, u32[]{:S(2)}) collective-permute-start(f32[256,1664]{1,0:T(8,128)} %fusion.105), channel_id=1, source_target_pairs={{0,4},{1,5},{2,6},{3,7},{4,0},{5,1},{6,2},{7,3},{8,12},{9,13},{10,... | collective-permute-start | bytes 5111816 | tf_op jit(solution)/shard_map/ppermute | solution.py:30
  815.0 28.3 %collective-permute-start = (f32[256,1664]{1,0:T(8,128)}, f32[256,1664]{1,0:T(8,128)}, u32[]{:S(2)}, u32[]{:S(2)}) collective-permute-start(f32[256,1664]{1,0:T(8,128)} %convolution_add_fusion.14), channel_id=1, source_target_pairs={{0,1},{1,0},{2,3},{3,2},{4,5},{5,4},{6,7},{7,6},{8,9},{9,8},{10,11... | collective-permute-start | bytes 5111816 | tf_op jit(solution)/shard_map/ppermute | solution.py:30
  816.0 55.9 %collective-permute-start.2 = (f32[256,1664]{1,0:T(8,128)}, f32[256,1664]{1,0:T(8,128)}, u32[]{:S(2)}, u32[]{:S(2)}) collective-permute-start(f32[256,1664]{1,0:T(8,128)} %fusion.103), channel_id=1, source_target_pairs={{0,4},{1,5},{2,6},{3,7},{4,0},{5,1},{6,2},{7,3},{8,12},{9,13},{10,... | collective-permute-start | bytes 5111816 | tf_op jit(solution)/shard_map/ppermute | solution.py:30
  820.9 60.6 %collective-permute-start.40 = (f32[640,1024]{1,0:T(8,128)}, f32[640,1024]{1,0:T(8,128)}, u32[]{:S(2)}, u32[]{:S(2)}) collective-permute-start(f32[640,1024]{1,0:T(8,128)} %get-tuple-element.90), channel_id=1, source_target_pairs={{0,1},{1,0},{2,3},{3,2},{4,5},{5,4},{6,7},{7,6},{8,9},{9,8},{10,11... | collective-permute-start | bytes 7864328 | tf_op jit(solution)/shard_map/ppermute | solution.py:30
  826.4 55.8 %collective-permute-start.24 = (f32[256,2560]{1,0:T(8,128)}, f32[256,2560]{1,0:T(8,128)}, u32[]{:S(2)}, u32[]{:S(2)}) collective-permute-start(f32[256,2560]{1,0:T(8,128)} %fusion.253), channel_id=1, source_target_pairs={{0,1},{1,0},{2,3},{3,2},{4,5},{5,4},{6,7},{7,6},{8,9},{9,8},{10,11... | collective-permute-start | bytes 7864328 | tf_op jit(solution)/shard_map/ppermute | solution.py:30
  843.3 57.4 %collective-permute-start.20 = (f32[256,2560]{1,0:T(8,128)}, f32[256,2560]{1,0:T(8,128)}, u32[]{:S(2)}, u32[]{:S(2)}) collective-permute-start(f32[256,2560]{1,0:T(8,128)} %fusion.259), channel_id=1, source_target_pairs={{0,1},{1,0},{2,3},{3,2},{4,5},{5,4},{6,7},{7,6},{8,9},{9,8},{10,11... | collective-permute-start | bytes 7864328 | tf_op jit(solution)/shard_map/ppermute | solution.py:30
  847.6 29.9 %collective-permute-start.13 = (f32[128,1664]{1,0:T(8,128)}, f32[128,1664]{1,0:T(8,128)}, u32[]{:S(2)}, u32[]{:S(2)}) collective-permute-start(f32[128,1664]{1,0:T(8,128)} %slice.609), channel_id=1, source_target_pairs={{0,2},{1,3},{2,0},{3,1},{4,6},{5,7},{6,4},{7,5},{8,10},{9,11},{10,... | collective-permute-start | bytes 2555912 | tf_op jit(solution)/shard_map/ppermute | solution.py:30
  871.9 45.3 %collective-permute-start.34 = (f32[256,2560]{1,0:T(8,128)}, f32[256,2560]{1,0:T(8,128)S(1)}, u32[]{:S(2)}, u32[]{:S(2)}) collective-permute-start(f32[256,2560]{1,0:T(8,128)} %fusion.241), channel_id=1, source_target_pairs={{0,1},{1,0},{2,3},{3,2},{4,5},{5,4},{6,7},{7,6},{8,9},{9,8},{10,11... | collective-permute-start | bytes 7864328 | tf_op jit(solution)/shard_map/ppermute | solution.py:30
  878.6 20.5 %collective-permute-start.3 = (f32[128,1664]{1,0:T(8,128)S(1)}, f32[128,1664]{1,0:T(8,128)S(1)}, u32[]{:S(2)}, u32[]{:S(2)}) collective-permute-start(f32[128,1664]{1,0:T(8,128)S(1)} %slice.588), channel_id=1, source_target_pairs={{0,2},{1,3},{2,0},{3,1},{4,6},{5,7},{6,4},{7,5},{8,10},{9,11},{10,... | collective-permute-start | bytes 2555912 | tf_op jit(solution)/shard_map/ppermute | solution.py:30
  881.5 58.5 %collective-permute-start.26 = (f32[256,2560]{1,0:T(8,128)S(1)}, f32[256,2560]{1,0:T(8,128)S(1)}, u32[]{:S(2)}, u32[]{:S(2)}) collective-permute-start(f32[256,2560]{1,0:T(8,128)S(1)} %copy-done.65), channel_id=1, source_target_pairs={{0,4},{1,5},{2,6},{3,7},{4,0},{5,1},{6,2},{7,3},{8,12},{9,13},{10,... | collective-permute-start | bytes 7864328 | tf_op jit(solution)/shard_map/ppermute | solution.py:30
  882.2 73.1 %collective-permute-start.22 = (f32[256,2560]{1,0:T(8,128)S(1)}, f32[256,2560]{1,0:T(8,128)S(1)}, u32[]{:S(2)}, u32[]{:S(2)}) collective-permute-start(f32[256,2560]{1,0:T(8,128)S(1)} %copy-done.66), channel_id=1, source_target_pairs={{0,2},{1,3},{2,0},{3,1},{4,6},{5,7},{6,4},{7,5},{8,10},{9,11},{10,... | collective-permute-start | bytes 7864328 | tf_op jit(solution)/shard_map/ppermute | solution.py:30
  899.1 97.2 %collective-permute-start.36 = (f32[256,2560]{1,0:T(8,128)}, f32[256,2560]{1,0:T(8,128)S(1)}, u32[]{:S(2)}, u32[]{:S(2)}) collective-permute-start(f32[256,2560]{1,0:T(8,128)} %convolution_add_fusion), channel_id=1, source_target_pairs={{0,4},{1,5},{2,6},{3,7},{4,0},{5,1},{6,2},{7,3},{8,12},{9,13},{10,... | collective-permute-start | bytes 7864328 | tf_op jit(solution)/shard_map/ppermute | solution.py:30
  900.7 15.4 %collective-permute-start.18 = (f32[64,2688]{1,0:T(8,128)S(1)}, f32[64,2688]{1,0:T(8,128)S(1)}, u32[]{:S(2)}, u32[]{:S(2)}) collective-permute-start(f32[64,2688]{1,0:T(8,128)S(1)} %pad_maximum_fusion.11), channel_id=1, source_target_pairs={{0,8},{1,9},{2,10},{3,11},{4,12},{5,13},{6,14},{7,15},{8,0},{9,1},... | collective-permute-start | bytes 2064392 | tf_op jit(solution)/shard_map/ppermute | solution.py:30
  917.2 99.8 %collective-permute-start.46 = (f32[640,1024]{1,0:T(8,128)}, f32[640,1024]{1,0:T(8,128)}, u32[]{:S(2)}, u32[]{:S(2)}) collective-permute-start(f32[640,1024]{1,0:T(8,128)} %get-tuple-element.92), channel_id=1, source_target_pairs={{0,1},{1,0},{2,3},{3,2},{4,5},{5,4},{6,7},{7,6},{8,9},{9,8},{10,11... | collective-permute-start | bytes 7864328 | tf_op jit(solution)/shard_map/ppermute | solution.py:30
  930.6 80.9 %collective-permute-start.42 = (f32[640,1024]{1,0:T(8,128)}, f32[640,1024]{1,0:T(8,128)}, u32[]{:S(2)}, u32[]{:S(2)}) collective-permute-start(f32[640,1024]{1,0:T(8,128)} %bitcast_add_fusion.3), channel_id=1, source_target_pairs={{0,2},{1,3},{2,0},{3,1},{4,6},{5,7},{6,4},{7,5},{8,10},{9,11},{10,... | collective-permute-start | bytes 7864328 | tf_op jit(solution)/shard_map/ppermute | solution.py:30
  940.0 127.7 %collective-permute-start.48 = (f32[640,1024]{1,0:T(8,128)}, f32[640,1024]{1,0:T(8,128)}, u32[]{:S(2)}, u32[]{:S(2)}) collective-permute-start(f32[640,1024]{1,0:T(8,128)} %bitcast_add_fusion.1), channel_id=1, source_target_pairs={{0,2},{1,3},{2,0},{3,1},{4,6},{5,7},{6,4},{7,5},{8,10},{9,11},{10,... | collective-permute-start | bytes 7864328 | tf_op jit(solution)/shard_map/ppermute | solution.py:30
  955.3 117.1 %collective-permute-start.30 = (f32[256,2560]{1,0:T(8,128)}, f32[256,2560]{1,0:T(8,128)}, u32[]{:S(2)}, u32[]{:S(2)}) collective-permute-start(f32[256,2560]{1,0:T(8,128)} %fusion.247), channel_id=1, source_target_pairs={{0,1},{1,0},{2,3},{3,2},{4,5},{5,4},{6,7},{7,6},{8,9},{9,8},{10,11... | collective-permute-start | bytes 7864328 | tf_op jit(solution)/shard_map/ppermute | solution.py:30
  997.8 126.1 %collective-permute-start.32 = (f32[256,2560]{1,0:T(8,128)}, f32[256,2560]{1,0:T(8,128)}, u32[]{:S(2)}, u32[]{:S(2)}) collective-permute-start(f32[256,2560]{1,0:T(8,128)} %convolution_add_fusion.2), channel_id=1, source_target_pairs={{0,2},{1,3},{2,0},{3,1},{4,6},{5,7},{6,4},{7,5},{8,10},{9,11},{10,... | collective-permute-start | bytes 7864328 | tf_op jit(solution)/shard_map/ppermute | solution.py:30
  1011.5 117.3 %collective-permute-start.19 = (f32[32,2688]{1,0:T(8,128)}, f32[32,2688]{1,0:T(8,128)S(1)}, u32[]{:S(2)}, u32[]{:S(2)}) collective-permute-start(f32[32,2688]{1,0:T(8,128)} %slice_add_fusion.10), channel_id=1, source_target_pairs={{0,16},{1,17},{2,18},{3,19},{4,20},{5,21},{6,22},{7,23},{8,24},{9,... | collective-permute-start | bytes 1032200 | tf_op jit(solution)/shard_map/ppermute | solution.py:30
  1017.0 112.9 %collective-permute-start.9 = (f32[32,2688]{1,0:T(8,128)}, f32[32,2688]{1,0:T(8,128)S(1)}, u32[]{:S(2)}, u32[]{:S(2)}) collective-permute-start(f32[32,2688]{1,0:T(8,128)} %slice_add_fusion.11), channel_id=1, source_target_pairs={{0,16},{1,17},{2,18},{3,19},{4,20},{5,21},{6,22},{7,23},{8,24},{9,... | collective-permute-start | bytes 1032200 | tf_op jit(solution)/shard_map/ppermute | solution.py:30
  1067.7 68.7 %collective-permute-start.43 = (f32[320,1024]{1,0:T(8,128)}, f32[320,1024]{1,0:T(8,128)S(1)}, u32[]{:S(2)}, u32[]{:S(2)}) collective-permute-start(f32[320,1024]{1,0:T(8,128)} %dynamic-slice_bitcast_fusion.5), channel_id=1, source_target_pairs={{0,4},{1,5},{2,6},{3,7},{4,0},{5,1},{6,2},{7,3},{8,12},{9,13},{10,... | collective-permute-start | bytes 3932168 | tf_op jit(solution)/shard_map/ppermute | solution.py:30
  1072.3 65.8 %collective-permute-start.49 = (f32[320,1024]{1,0:T(8,128)S(1)}, f32[320,1024]{1,0:T(8,128)S(1)}, u32[]{:S(2)}, u32[]{:S(2)}) collective-permute-start(f32[320,1024]{1,0:T(8,128)S(1)} %dynamic-slice_bitcast_fusion.4), channel_id=1, source_target_pairs={{0,4},{1,5},{2,6},{3,7},{4,0},{5,1},{6,2},{7,3},{8,12},{9,13},{10,... | collective-permute-start | bytes 3932168 | tf_op jit(solution)/shard_map/ppermute | solution.py:30
  1123.9 29.5 %collective-permute-start.27 = (f32[128,2560]{1,0:T(8,128)S(1)}, f32[128,2560]{1,0:T(8,128)S(1)}, u32[]{:S(2)}, u32[]{:S(2)}) collective-permute-start(f32[128,2560]{1,0:T(8,128)S(1)} %slice.644), channel_id=1, source_target_pairs={{0,2},{1,3},{2,0},{3,1},{4,6},{5,7},{6,4},{7,5},{8,10},{9,11},{10,... | collective-permute-start | bytes 3932168 | tf_op jit(solution)/shard_map/ppermute | solution.py:30
  1128.9 29.3 %collective-permute-start.23 = (f32[128,2560]{1,0:T(8,128)S(1)}, f32[128,2560]{1,0:T(8,128)S(1)}, u32[]{:S(2)}, u32[]{:S(2)}) collective-permute-start(f32[128,2560]{1,0:T(8,128)S(1)} %slice.638), channel_id=1, source_target_pairs={{0,4},{1,5},{2,6},{3,7},{4,0},{5,1},{6,2},{7,3},{8,12},{9,13},{10,... | collective-permute-start | bytes 3932168 | tf_op jit(solution)/shard_map/ppermute | solution.py:30
  1129.9 51.6 %collective-permute-start.37 = (f32[128,2560]{1,0:T(8,128)S(1)}, f32[128,2560]{1,0:T(8,128)S(1)}, u32[]{:S(2)}, u32[]{:S(2)}) collective-permute-start(f32[128,2560]{1,0:T(8,128)S(1)} %slice.665), channel_id=1, source_target_pairs={{0,2},{1,3},{2,0},{3,1},{4,6},{5,7},{6,4},{7,5},{8,10},{9,11},{10,... | collective-permute-start | bytes 3932168 | tf_op jit(solution)/shard_map/ppermute | solution.py:30
  1136.4 49.8 %collective-permute-start.33 = (f32[128,2560]{1,0:T(8,128)S(1)}, f32[128,2560]{1,0:T(8,128)S(1)}, u32[]{:S(2)}, u32[]{:S(2)}) collective-permute-start(f32[128,2560]{1,0:T(8,128)S(1)} %slice.659), channel_id=1, source_target_pairs={{0,4},{1,5},{2,6},{3,7},{4,0},{5,1},{6,2},{7,3},{8,12},{9,13},{10,... | collective-permute-start | bytes 3932168 | tf_op jit(solution)/shard_map/ppermute | solution.py:30
  1138.1 48.3 %collective-permute-start.44 = (f32[160,1024]{1,0:T(8,128)S(1)}, f32[160,1024]{1,0:T(8,128)S(1)}, u32[]{:S(2)}, u32[]{:S(2)}) collective-permute-start(f32[160,1024]{1,0:T(8,128)S(1)} %pad_maximum_fusion.18), channel_id=1, source_target_pairs={{0,8},{1,9},{2,10},{3,11},{4,12},{5,13},{6,14},{7,15},{8,0},{9,1},... | collective-permute-start | bytes 1966088 | tf_op jit(solution)/shard_map/ppermute | solution.py:30
  1153.4 33.2 %collective-permute-start.50 = (f32[160,1024]{1,0:T(8,128)S(1)}, f32[160,1024]{1,0:T(8,128)S(1)}, u32[]{:S(2)}, u32[]{:S(2)}) collective-permute-start(f32[160,1024]{1,0:T(8,128)S(1)} %pad_maximum_fusion.19), channel_id=1, source_target_pairs={{0,8},{1,9},{2,10},{3,11},{4,12},{5,13},{6,14},{7,15},{8,0},{9,1},... | collective-permute-start | bytes 1966088 | tf_op jit(solution)/shard_map/ppermute | solution.py:30
  1158.5 60.7 %collective-permute-start.28 = (f32[64,5120]{1,0:T(8,128)S(1)}, f32[64,5120]{1,0:T(8,128)S(1)}, u32[]{:S(2)}, u32[]{:S(2)}) collective-permute-start(f32[64,5120]{1,0:T(8,128)S(1)} %pad_maximum_fusion.4), channel_id=1, source_target_pairs={{0,8},{1,9},{2,10},{3,11},{4,12},{5,13},{6,14},{7,15},{8,0},{9,1},... | collective-permute-start | bytes 3932168 | tf_op jit(solution)/shard_map/ppermute | solution.py:30
  1186.7 29.3 %collective-permute-start.51 = (f32[80,1024]{1,0:T(8,128)S(1)}, f32[80,1024]{1,0:T(8,128)S(1)}, u32[]{:S(2)}, u32[]{:S(2)}) collective-permute-start(f32[80,1024]{1,0:T(8,128)S(1)} %slice_add_fusion.12), channel_id=1, source_target_pairs={{0,16},{1,17},{2,18},{3,19},{4,20},{5,21},{6,22},{7,23},{8,24},{9,... | collective-permute-start | bytes 983048 | tf_op jit(solution)/shard_map/ppermute | solution.py:30
  1189.2 61.7 %collective-permute-start.38 = (f32[64,5120]{1,0:T(8,128)S(1)}, f32[64,5120]{1,0:T(8,128)S(1)}, u32[]{:S(2)}, u32[]{:S(2)}) collective-permute-start(f32[64,5120]{1,0:T(8,128)S(1)} %pad_maximum_fusion.5), channel_id=1, source_target_pairs={{0,8},{1,9},{2,10},{3,11},{4,12},{5,13},{6,14},{7,15},{8,0},{9,1},... | collective-permute-start | bytes 3932168 | tf_op jit(solution)/shard_map/ppermute | solution.py:30
  1219.2 31.8 %collective-permute-start.29 = (f32[32,5120]{1,0:T(8,128)S(1)}, f32[32,5120]{1,0:T(8,128)S(1)}, u32[]{:S(2)}, u32[]{:S(2)}) collective-permute-start(f32[32,5120]{1,0:T(8,128)S(1)} %slice_add_fusion.7), channel_id=1, source_target_pairs={{0,16},{1,17},{2,18},{3,19},{4,20},{5,21},{6,22},{7,23},{8,24},{9,... | collective-permute-start | bytes 1966088 | tf_op jit(solution)/shard_map/ppermute | solution.py:30
  1251.0 30.6 %collective-permute-start.39 = (f32[32,5120]{1,0:T(8,128)S(1)}, f32[32,5120]{1,0:T(8,128)S(1)}, u32[]{:S(2)}, u32[]{:S(2)}) collective-permute-start(f32[32,5120]{1,0:T(8,128)S(1)} %slice_add_fusion.6), channel_id=1, source_target_pairs={{0,16},{1,17},{2,18},{3,19},{4,20},{5,21},{6,22},{7,23},{8,24},{9,... | collective-permute-start | bytes 1966088 | tf_op jit(solution)/shard_map/ppermute | solution.py:30
  (186 other events, 2624.0 us)
